TPU v7x, 32 devices: a whole 2x2x4 slice. The times are simulated.
32 devices in a mesh: dom: 32 (over z, y, x, core).
Axes of the slice: x: 2, y: 2, z: 4, core: 2. Of those that a mesh axis runs over, the one named last changes fastest.
Arguments:
- features: bfloat16 [8192, 512], P('dom'), may hold values from -6 to 6
- w_one: bfloat16 [9, 512, 512], replicated, may hold values from -0.25 to 0.25
- w_two: bfloat16 [8, 512, 349], replicated, may hold values from -0.25 to 0.25
- self_two: bfloat16 [512, 349], replicated, may hold values from -80 to 80
- edge_src: int32 [8, 64, 256], P(None, 'dom'), may hold values from 0 to 511, as said below
- edge_dst: int32 [8, 64, 256], P(None, 'dom'), may hold values from -1 to 127, as said below
- send_rows: int32 [32, 32, 8], P('dom'), may hold values from 0 to 255
- send_count: int32 [32, 32], P('dom'), may hold values from 1 to 8, as said below
- labels: int32 [8192], P('dom'), may hold values from -1 to 348
Outputs:
- logits: float32 [8192, 349], P('dom')
- loss: float32 [], replicated
- grad_one: float32 [4608, 512], P('dom')
- grad_two: float32 [4608, 349], P('dom')
Inputs may be any that keep to these rules, and one draw needn't show every extreme that they name: `send_rows`: entry [p, q, s] is a row of partition p's own nodes, rows may repeat. `send_count`: entry [p, q] counts the live slots p sends to q; every row reaches 8 at some q. `edge_src`: index into the destination partition's table: its 256 own rows, then 8 slots from each partition in order. `edge_dst`: -1 marks an empty edge slot.
All inputs are finite; a program needn't handle non-finite values.
Results may differ from a plain program's by a relative error of at most 0.0085.
The roundings to bfloat16 on the way count: a program that leaves them out, or rounds other values in their place, can miss the bound.
Values may be sent and summed in bfloat16 or wider, within the bound.
A program may use at most 128 MiB of HBM per device.

v0:
```python
import jax
import jax.numpy as jnp
from jax import lax
from jax.sharding import PartitionSpec as P

loss_scale = 256.0


def pack_rows(values, picks, live_slot):
    chosen = values[picks]
    return jnp.where(live_slot[:, :, None], chosen, jnp.zeros_like(chosen))


def aggregate(node_table, sources, targets):
    blocks = sources.shape[1]
    block_rows = jnp.arange(128, dtype=jnp.int32)

    def one_relation(edge_pair):
        src_rel, dst_rel = edge_pair
        picked = node_table[src_rel]
        one_hot = dst_rel[:, None, :] == block_rows[None, :, None]
        sums = jnp.einsum(
            "bve,bed->bvd", one_hot.astype(jnp.bfloat16), picked, preferred_element_type=jnp.float32
        )
        counts = jnp.sum(one_hot.astype(jnp.float32), axis=2)
        norm_rows = 1.0 / jnp.maximum(counts, 1.0)
        averaged = (sums * norm_rows[:, :, None]).astype(jnp.bfloat16)
        return (averaged.reshape(blocks * 128, -1), norm_rows.reshape(blocks * 128))

    return lax.map(one_relation, (sources, targets))


def spread_back(spread, sources, targets, table_rows):
    blocks = sources.shape[1]
    block_rows = jnp.arange(128, dtype=jnp.int32)

    def add_relation(total, edge_pack):
        grad_rel, src_rel, dst_rel = edge_pack
        one_hot = (dst_rel[:, None, :] == block_rows[None, :, None]).astype(jnp.bfloat16)
        per_edge = jnp.einsum(
            "bve,bvd->bed",
            one_hot,
            grad_rel.reshape(blocks, 128, -1),
            preferred_element_type=jnp.float32,
        )
        added = jax.ops.segment_sum(
            per_edge.reshape(-1, per_edge.shape[-1]), src_rel.reshape(-1), num_segments=table_rows
        )
        return (total + added, None)

    start = jnp.zeros((table_rows, spread.shape[-1]), jnp.float32)
    total, unused = lax.scan(add_relation, start, (spread, sources, targets))
    return total


def stacked_rows(averaged, own_rows):
    stacked = jnp.concatenate([averaged, own_rows[None]], axis=0)
    return jnp.swapaxes(stacked, 1, 2).reshape(-1, stacked.shape[1])


def on_device(features, w_one, w_two, self_two, edge_src, edge_dst, send_rows, send_count, labels):
    peers = lax.axis_size("dom")
    node_rows = features.shape[0]
    width = features.shape[1]
    relations = w_two.shape[0]
    picks = send_rows[0]
    slots = picks.shape[1]
    live_slot = jnp.arange(slots, dtype=jnp.int32)[None, :] < send_count[0][:, None]
    table_rows = node_rows + peers * slots
    arrived = lax.all_to_all(
        pack_rows(features, picks, live_slot), "dom", split_axis=0, concat_axis=0, tiled=True
    )
    node_table = jnp.concatenate([features, arrived.reshape(peers * slots, width)], axis=0)
    averaged_one, norm_one = aggregate(node_table, edge_src, edge_dst)
    before_relu = jnp.einsum(
        "rnd,rde->ne", averaged_one, w_one[:relations], preferred_element_type=jnp.float32
    )
    before_relu = before_relu + jnp.dot(
        features, w_one[relations], preferred_element_type=jnp.float32
    )
    hidden = jnp.maximum(before_relu, 0.0).astype(jnp.bfloat16)
    arrived_hidden = lax.all_to_all(
        pack_rows(hidden, picks, live_slot), "dom", split_axis=0, concat_axis=0, tiled=True
    )
    hidden_table = jnp.concatenate([hidden, arrived_hidden.reshape(peers * slots, width)], axis=0)
    averaged_two, norm_two = aggregate(hidden_table, edge_src, edge_dst)
    logits = jnp.einsum("rnd,rdc->nc", averaged_two, w_two, preferred_element_type=jnp.float32)
    logits = logits + jnp.dot(hidden, self_two, preferred_element_type=jnp.float32)
    classes = logits.shape[1]
    labelled = labels >= 0
    log_total = jax.nn.logsumexp(logits, axis=1)
    one_hot = (jnp.arange(classes, dtype=jnp.int32)[None, :] == labels[:, None]).astype(jnp.float32)
    picked = jnp.sum(logits * one_hot, axis=1)
    local_total = jnp.sum(jnp.where(labelled, log_total - picked, 0.0))
    local_count = jnp.sum(labelled.astype(jnp.float32))
    total, label_count = lax.psum((local_total, local_count), "dom")
    loss = total / label_count
    softmax_out = jnp.exp(logits - log_total[:, None])
    grad_logits = (
        loss_scale * (softmax_out - one_hot) * labelled[:, None].astype(jnp.float32) / label_count
    ).astype(jnp.bfloat16)
    left_two = stacked_rows(averaged_two, hidden)
    grad_two = lax.psum_scatter(
        jnp.dot(left_two, grad_logits, preferred_element_type=jnp.float32),
        "dom",
        scatter_dimension=0,
        tiled=True,
    )
    spread = jnp.einsum("nc,rdc->rnd", grad_logits, w_two, preferred_element_type=jnp.float32)
    spread = (spread * norm_two[:, :, None]).astype(jnp.bfloat16)
    table_grad = spread_back(spread, edge_src, edge_dst, table_rows)
    local_grad = table_grad[:node_rows] + jnp.dot(
        grad_logits, self_two.T, preferred_element_type=jnp.float32
    )
    outgoing = table_grad[node_rows:].astype(jnp.bfloat16).reshape(peers, slots, width)
    returned = lax.all_to_all(outgoing, "dom", split_axis=0, concat_axis=0, tiled=True)
    returned = jnp.where(live_slot[:, :, None], returned.astype(jnp.float32), 0.0)
    grad_hidden = local_grad + jax.ops.segment_sum(
        returned.reshape(peers * slots, width), picks.reshape(-1), num_segments=node_rows
    )
    grad_pre = jnp.where(before_relu > 0.0, grad_hidden, 0.0).astype(jnp.bfloat16)
    left_one = stacked_rows(averaged_one, features)
    grad_one = lax.psum_scatter(
        jnp.dot(left_one, grad_pre, preferred_element_type=jnp.float32),
        "dom",
        scatter_dimension=0,
        tiled=True,
    )
    return (logits, loss, grad_one, grad_two)


def solution(mesh):
    in_specs = (
        P("dom", None),
        P(),
        P(),
        P(),
        P(None, "dom", None),
        P(None, "dom", None),
        P("dom", None, None),
        P("dom", None),
        P("dom"),
    )
    out_specs = (P("dom", None), P(), P("dom", None), P("dom", None))
    return jax.shard_map(
        on_device, mesh=mesh, in_specs=in_specs, out_specs=out_specs, check_vma=False
    )
```

profile of v0, /device:TPU:0, one launch (start us, length us, event | category | flops | bytes accessed | tf_op | source)
XLA Modules:
  0.0 483.7 jit_solution(15193342183866101057)
XLA Ops:
  11.9 7.3 %all-to-all-start = ((bf16[32,8,512]{2,1,0:T(8,128)(2,1)}), bf16[32,8,512]{2,1,0:T(8,128)(2,1)S(1)}, u32[]{:S(2)}, u32[]{:S(2)}) async-start(bf16[32,8,512]{2,1,0:T(8,128)(2,1)} %bitcast_select_fusion.1), calls=%async_computation | async-start | bytes 524288 | tf_op jit(solution)/shard_map/all_to_all | solution.py:70
  19.3 10.6 %all-to-all-done = bf16[32,8,512]{2,1,0:T(8,128)(2,1)S(1)} async-done(((bf16[32,8,512]{2,1,0:T(8,128)(2,1)}), bf16[32,8,512]{2,1,0:T(8,128)(2,1)S(1)}, u32[]{:S(2)}, u32[]{:S(2)}) %all-to-all-start) | async-done | bytes 262176 | tf_op jit(solution)/shard_map/all_to_all | solution.py:70
  33.1 49.1 %while.35 = (s32[]{:T(128)}, bf16[8,256,512]{2,1,0:T(8,128)(2,1)}, s32[8,2,256]{2,1,0:T(2,128)}, s32[8,2,256]{2,1,0:T(2,128)}, bf16[512,512]{1,0:T(8,128)(2,1)S(1)}, /*index=5*/s32[]{:T(128)}) while((s32[]{:T(128)}, bf16[8,256,512]{2,1,0:T(8,128)(2,1)}, s32[8,2,256]{2,1,0:T(2,128)}, s32[8,2,256]{2,1,0:T(2,128)}, ...), condition=%wide.region_2.3_spmd.clone, body=%wide.region_0.2_spmd.clone.sunk | while | flops 67635968 | bytes 2388057 | solution.py:30
  82.3 4.1 fusion.27
  94.0 9.6 %all-to-all-done.1 = bf16[32,8,512]{2,1,0:T(8,128)(2,1)S(1)} async-done(((bf16[32,8,512]{2,1,0:T(8,128)(2,1)}), bf16[32,8,512]{2,1,0:T(8,128)(2,1)S(1)}, u32[]{:S(2)}, u32[]{:S(2)}) %all-to-all-start.1) | async-done | bytes 262176 | tf_op jit(solution)/shard_map/all_to_all | solution.py:82
  107.0 49.6 %while.36 = (s32[]{:T(128)}, bf16[8,256,512]{2,1,0:T(8,128)(2,1)}, f32[8,256]{1,0:T(8,128)S(1)}, s32[8,2,256]{2,1,0:T(2,128)}, s32[8,2,256]{2,1,0:T(2,128)}, /*i...) while((s32[]{:T(128)}, bf16[8,256,512]{2,1,0:T(8,128)(2,1)}, f32[8,256]{1,0:T(8,128)S(1)}, ...), condition=%wide.region_5.6_spmd.clone, body=%wide.region_3.5_spmd.clone.sunk | while | flops 67635968 | bytes 2390125 | solution.py:30
  166.7 39.0 %all-reduce = (f32[]{:T(128)}, f32[]{:T(128)}) all-reduce(f32[]{:T(128)} %get-tuple-element.151, f32[]{:T(128)} %get-tuple-element.150), channel_id=1, replica_groups=mesh['dom'=32] {'dom'}, use_global_device_ids=true, to_apply=%region_10.11 | all-reduce | flops 2 | bytes 16 | tf_op jit(solution)/shard_map/psum | solution.py:96
  205.7 6.5 %fusion.46 = f32[4608,349]{1,0:T(8,128)} fusion(bf16[4608,256]{1,0:T(8,128)(2,1)} %bitcast.132, f32[256,349]{0,1:T(8,128)S(1)} %get-tuple-element.191, f32[]{:T(128)} %get-tuple-element.185, f32[256]{0:T(256)S(1)} %get-tuple-element.187, f32[256]{0:T(256)S(1)} %get-tuple-element.186, s32[256]{0:T(256)S(1)} %copy-done.15), kind=kOutput, calls=%fused_computation.87 | convolution fusion | flops 824019712 | bytes 9152516 | tf_op jit(solution)/shard_map/dot_general | solution.py:104
  212.3 4.0 fusion.18
  217.4 81.5 %while.37 = (s32[]{:T(128)}, f32[512,512]{1,0:T(8,128)}, s32[8,2,256]{2,1,0:T(2,128)}, s32[8,2,256]{2,1,0:T(2,128)}, bf16[8,256,512]{2,1,0:T(8,128)(2,1)}, /*index=5*/s32[]{:T(128)}) while((s32[]{:T(128)}, f32[512,512]{1,0:T(8,128)}, s32[8,2,256]{2,1,0:T(2,128)}, s32[8,2,256]{2,1,0:T(2,128)}, bf16[8,256,512]{2,1,0:T(8,128)(2,1)}, ...), condition=%wide.region_15.16_spmd.clone, body=%wide.region_13.15_spmd.clone.sunk | while | flops 67436544 | bytes 4997209 | solution.py:52
  221.2 6.5 %scatter_fusion = f32[512,512]{1,0:T(8,128)} fusion(f32[512,512]{1,0:T(8,128)} %get-tuple-element.340, s32[512]{0:T(512)S(1)} %bitcast.138, f32[512,512]{1,0:T(8,128)} %bitcast.125), kind=kCustom, calls=%fused_computation.4.clone.clone.1 | custom fusion | flops 262144 | bytes 3147776 | tf_op jit(solution)/shard_map/while/body/eval_jaxpr/scatter-add | solution.py:46
  231.4 6.5 %scatter_fusion = f32[512,512]{1,0:T(8,128)} fusion(f32[512,512]{1,0:T(8,128)} %get-tuple-element.340, s32[512]{0:T(512)S(1)} %bitcast.138, f32[512,512]{1,0:T(8,128)} %bitcast.125), kind=kCustom, calls=%fused_computation.4.clone.clone.1 | custom fusion | flops 262144 | bytes 3147776 | tf_op jit(solution)/shard_map/while/body/eval_jaxpr/scatter-add | solution.py:46
  241.6 6.5 %scatter_fusion = f32[512,512]{1,0:T(8,128)} fusion(f32[512,512]{1,0:T(8,128)} %get-tuple-element.340, s32[512]{0:T(512)S(1)} %bitcast.138, f32[512,512]{1,0:T(8,128)} %bitcast.125), kind=kCustom, calls=%fused_computation.4.clone.clone.1 | custom fusion | flops 262144 | bytes 3147776 | tf_op jit(solution)/shard_map/while/body/eval_jaxpr/scatter-add | solution.py:46
  251.8 6.5 %scatter_fusion = f32[512,512]{1,0:T(8,128)} fusion(f32[512,512]{1,0:T(8,128)} %get-tuple-element.340, s32[512]{0:T(512)S(1)} %bitcast.138, f32[512,512]{1,0:T(8,128)} %bitcast.125), kind=kCustom, calls=%fused_computation.4.clone.clone.1 | custom fusion | flops 262144 | bytes 3147776 | tf_op jit(solution)/shard_map/while/body/eval_jaxpr/scatter-add | solution.py:46
  261.9 6.7 %scatter_fusion = f32[512,512]{1,0:T(8,128)} fusion(f32[512,512]{1,0:T(8,128)} %get-tuple-element.340, s32[512]{0:T(512)S(1)} %bitcast.138, f32[512,512]{1,0:T(8,128)} %bitcast.125), kind=kCustom, calls=%fused_computation.4.clone.clone.1 | custom fusion | flops 262144 | bytes 3147776 | tf_op jit(solution)/shard_map/while/body/eval_jaxpr/scatter-add | solution.py:46
  272.3 6.4 %scatter_fusion = f32[512,512]{1,0:T(8,128)} fusion(f32[512,512]{1,0:T(8,128)} %get-tuple-element.340, s32[512]{0:T(512)S(1)} %bitcast.138, f32[512,512]{1,0:T(8,128)} %bitcast.125), kind=kCustom, calls=%fused_computation.4.clone.clone.1 | custom fusion | flops 262144 | bytes 3147776 | tf_op jit(solution)/shard_map/while/body/eval_jaxpr/scatter-add | solution.py:46
  282.4 6.4 %scatter_fusion = f32[512,512]{1,0:T(8,128)} fusion(f32[512,512]{1,0:T(8,128)} %get-tuple-element.340, s32[512]{0:T(512)S(1)} %bitcast.138, f32[512,512]{1,0:T(8,128)} %bitcast.125), kind=kCustom, calls=%fused_computation.4.clone.clone.1 | custom fusion | flops 262144 | bytes 3147776 | tf_op jit(solution)/shard_map/while/body/eval_jaxpr/scatter-add | solution.py:46
  292.5 6.5 %scatter_fusion = f32[512,512]{1,0:T(8,128)} fusion(f32[512,512]{1,0:T(8,128)} %get-tuple-element.340, s32[512]{0:T(512)S(1)} %bitcast.138, f32[512,512]{1,0:T(8,128)} %bitcast.125), kind=kCustom, calls=%fused_computation.4.clone.clone.1 | custom fusion | flops 262144 | bytes 3147776 | tf_op jit(solution)/shard_map/while/body/eval_jaxpr/scatter-add | solution.py:46
  300.7 4.0 all-to-all-start.2
  305.8 4.0 copy.18
  317.4 4.4 scatter_custom_fusion.1
  321.8 6.9 %fusion.39 = f32[4608,512]{1,0:T(8,128)} fusion(bf16[4608,256]{1,0:T(8,128)(2,1)} %bitcast.133, f32[256,512]{1,0:T(8,128)} %scatter_custom_fusion.1, f32[256,512]{1,0:T(8,128)} %get-tuple-element.189), kind=kOutput, calls=%fused_computation.69 | convolution fusion | flops 1208221696 | bytes 12845056 | tf_op jit(solution)/shard_map/dot_general | solution.py:124
  329.9 4.2 reduce-scatter.5.cloned.1.call-done
  334.1 141.6 %reduce-scatter.3.cloned.1.call-done = f32[144,512]{1,0:T(8,128)} async-done(((f32[4608,512]{1,0:T(8,128)}), f32[144,512]{1,0:T(8,128)}) %reduce-scatter.3.cloned.1.call-update) | async-done | bytes 294928 | tf_op jit(solution)/shard_map/reduce_scatter | solution.py:123
  (260 shorter events, 168.6 us)
Async XLA Ops:
  7.2 153.3 %copy-start = (bf16[8,512,349]{1,0,2:T(8,128)(2,1)S(1)}, bf16[8,512,349]{1,0,2:T(8,128)(2,1)}, u32[]{:S(2)}) copy-start(bf16[8,512,349]{1,0,2:T(8,128)(2,1)} %param.17) | copy-start | bytes 8577028
  11.9 17.9 %all-to-all-start = ((bf16[32,8,512]{2,1,0:T(8,128)(2,1)}), bf16[32,8,512]{2,1,0:T(8,128)(2,1)S(1)}, u32[]{:S(2)}, u32[]{:S(2)}) async-start(bf16[32,8,512]{2,1,0:T(8,128)(2,1)} %bitcast_select_fusion.1), calls=%async_computation | async-start | bytes 524288 | tf_op jit(solution)/shard_map/all_to_all | solution.py:70
  29.8 0.7 copy-start.11
  82.3 4.1 copy-start.4
  88.5 15.1 %copy-start.2 = (bf16[256,512]{1,0:T(8,128)(2,1)}, bf16[256,512]{1,0:T(8,128)(2,1)S(1)}, u32[]{:S(2)}) copy-start(bf16[256,512]{1,0:T(8,128)(2,1)S(1)} %get-tuple-element.188) | copy-start | bytes 786436
  90.5 13.2 %all-to-all-start.1 = ((bf16[32,8,512]{2,1,0:T(8,128)(2,1)}), bf16[32,8,512]{2,1,0:T(8,128)(2,1)S(1)}, u32[]{:S(2)}, u32[]{:S(2)}) async-start(bf16[32,8,512]{2,1,0:T(8,128)(2,1)} %bitcast_select_fusion), calls=%async_computation.1 | async-start | bytes 524288 | tf_op jit(solution)/shard_map/all_to_all | solution.py:82
  93.1 241.1 %reduce-scatter.5.cloned.1.call-start = ((), (), s32[]{:S(2)}) async-start(), calls=%async_computation.6 | async-start | bytes 7299072 | tf_op jit(solution)/shard_map/reduce_scatter | solution.py:103
  103.7 0.7 copy-start.10
  160.5 3.5 copy-start.3
  160.5 3.5 copy-start.12
  160.5 3.9 copy-start.6
  160.5 3.9 copy-start.8
  164.3 148.8 %copy-start.7 = (f32[256,349]{0,1:T(8,128)}, f32[256,349]{0,1:T(8,128)S(1)}, u32[]{:S(2)}) copy-start(f32[256,349]{0,1:T(8,128)S(1)} %get-tuple-element.191) | copy-start | bytes 1072132
  164.4 1.6 copy-start.15
  217.4 87.4 %copy-start.14 = (s32[1,32,8]{1,2,0:T(8,128)S(1)}, s32[1,32,8]{1,2,0:T(8,128)}, u32[]{:S(2)}) copy-start(s32[1,32,8]{1,2,0:T(8,128)} %param.21) | copy-start | bytes 3076
  217.4 87.5 %copy-start.5 = (bf16[256,512]{1,0:T(8,128)(2,1)S(1)}, bf16[256,512]{1,0:T(8,128)(2,1)}, u32[]{:S(2)}) copy-start(bf16[256,512]{1,0:T(8,128)(2,1)} %param.15) | copy-start | bytes 786436
  300.7 16.7 %all-to-all-start.2 = ((bf16[32,8,512]{2,1,0:T(8,128)(2,1)}), bf16[32,8,512]{2,1,0:T(8,128)(2,1)}, u32[]{:S(2)}, u32[]{:S(2)}) async-start(bf16[32,8,512]{2,1,0:T(8,128)(2,1)} %fusion.40), calls=%async_computation.2 | async-start | bytes 524288 | tf_op jit(solution)/shard_map/all_to_all | solution.py:116
  304.8 171.0 %reduce-scatter.3.cloned.1.call-start = ((), (), s32[]{:S(2)}) async-start(), calls=%async_computation.5 | async-start | bytes 9732096 | tf_op jit(solution)/shard_map/reduce_scatter | solution.py:123
  305.7 4.1 copy-start.9
  309.8 3.3 copy-start.1
  309.8 3.3 copy-start.13
Sparse Core Ops, SparseCore 0:
  212.4 121.6 reduce-scatter.4
  340.6 135.0 reduce-scatter.2
where the time goes:
time: 487 us; the launch traced here: 484 us
  waiting for transfers between devices  169 us (35%)
  local copies, waits for them, and re-layouts  104 us (21%)
  other arithmetic  80.5 us (17%)
  matrix products  60.4 us (12%)
  blocking collectives  39 us (8%)
  between operations  16.5 us (3%)
  starting transfers between devices  14 us (3%)
    reduce_scatter x1, waiting for transfers between devices, on_device(): lax.psum_scatter(jnp.dot(left_one, grad_pre, preferred_element_type=jnp.f...  142 us
    scatter-add x8, other arithmetic, add_relation(): jax.ops.segment_sum(per_edge.reshape(-1, per_edge.shape[-1]), src_rel.res...  52 us
    gather x16, local copies, waits for them, and re-layouts, one_relation(): picked = node_table[src_rel]  42 us
    psum x1, blocking collectives, on_device(): total, label_count = lax.psum((local_total, local_count), 'dom')  39 us
    dot_general x16, matrix products, one_relation(): jnp.einsum('bve,bed->bvd', one_hot.astype(jnp.bfloat16), picked, preferre...  20.4 us
    dynamic_update_slice x24, local copies, waits for them, and re-layouts, aggregate(): return lax.map(one_relation, (sources, targets))  12 us
    while x16, other arithmetic  11 us
    eq x16, local copies, waits for them, and re-layouts, one_relation(): one_hot = dst_rel[:, None, :] == block_rows[None, :, None]  10.9 us
  transfers between devices with their start and end apart: 5, of which 5 were waited for; matrix products, arithmetic and copies ran while one was open for 23% of the time, Pallas kernels for 0%

commit v1 on v0

v1 whole, which is shorter than its diff:
```python
import jax
import jax.numpy as jnp
from jax import lax
from jax.sharding import PartitionSpec as P

loss_scale = 256.0
f32 = jnp.float32
bf16 = jnp.bfloat16


def exchange(rows, peers, slots):
    sent = rows.reshape(peers, slots, -1)
    got = lax.all_to_all(sent, "dom", split_axis=0, concat_axis=0, tiled=True)
    return got.reshape(peers * slots, -1)


def all_sum(value):
    spread = jnp.broadcast_to(value, (1, 128))
    return jnp.sum(lax.all_gather(spread, "dom", axis=0, tiled=True)[:, 0])


def on_device(features, w_one, w_two, self_two, edge_src, edge_dst, send_rows, send_count, labels):
    peers = lax.axis_size("dom")
    node_rows, width = features.shape
    relations, blocks, edges = edge_src.shape
    slots = send_rows.shape[2]
    table_rows = node_rows + peers * slots
    labelled = labels >= 0
    label_count = all_sum(jnp.sum(labelled.astype(f32)))

    live = jnp.arange(slots, dtype=jnp.int32)[None, :] < send_count[0][:, None]
    picks = jnp.where(live, send_rows[0], -1).reshape(-1)
    select = (picks[:, None] == jnp.arange(node_rows, dtype=jnp.int32)[None, :]).astype(bf16)

    arrived = exchange(jnp.dot(select, features), peers, slots)
    hot_dst = edge_dst[:, :, None, :] == jnp.arange(128, dtype=jnp.int32)[None, None, :, None]
    hot_src = edge_src[:, :, None, :] == jnp.arange(table_rows, dtype=jnp.int32)[None, None, :, None]
    counts = jnp.einsum(
        "rbve,rbte->rbvt", hot_dst.astype(bf16), hot_src.astype(bf16), preferred_element_type=f32
    )
    adj = counts.astype(bf16).reshape(relations * blocks * 128, table_rows)
    norm = 1.0 / jnp.maximum(jnp.sum(hot_dst.astype(f32), axis=3), 1.0)
    norm = norm.reshape(relations * blocks * 128, 1)

    def averages(own, got):
        table = jnp.concatenate([own, got], axis=0)
        sums = jnp.dot(adj, table, preferred_element_type=f32)
        return (sums * norm).astype(bf16).reshape(relations, node_rows, width)

    avg_one = jnp.concatenate([averages(features, arrived), features[None]], axis=0)
    pre = jnp.einsum("rnd,rde->ne", avg_one, w_one, preferred_element_type=f32)
    hidden = jnp.maximum(pre, 0.0).astype(bf16)
    arrived_hidden = exchange(jnp.dot(select, hidden), peers, slots)
    avg_two = jnp.concatenate([averages(hidden, arrived_hidden), hidden[None]], axis=0)
    w_all = jnp.concatenate([w_two, self_two[None]], axis=0)
    logits = jnp.einsum("rnd,rdc->nc", avg_two, w_all, preferred_element_type=f32)

    classes = logits.shape[1]
    log_total = jax.nn.logsumexp(logits, axis=1)
    one_hot = (jnp.arange(classes, dtype=jnp.int32)[None, :] == labels[:, None]).astype(f32)
    picked = jnp.sum(logits * one_hot, axis=1)
    local_total = jnp.sum(jnp.where(labelled, log_total - picked, 0.0))
    softmax_out = jnp.exp(logits - log_total[:, None])
    grad_logits = (
        loss_scale * (softmax_out - one_hot) * labelled[:, None].astype(f32) / label_count
    ).astype(bf16)

    def scattered(left, right):
        full = jnp.einsum("rnd,nc->rdc", left, right, preferred_element_type=f32)
        full = full.astype(bf16).reshape((relations + 1) * width, -1)
        return lax.psum_scatter(full, "dom", scatter_dimension=0, tiled=True).astype(f32)

    grad_two = scattered(avg_two, grad_logits)
    spread = jnp.einsum("nc,rdc->rnd", grad_logits, w_two, preferred_element_type=f32)
    spread = (spread.reshape(-1, width) * norm).astype(bf16)
    table_grad = lax.dot_general(adj, spread, (((0,), (0,)), ((), ())), preferred_element_type=f32)
    local_grad = table_grad[:node_rows] + jnp.dot(
        grad_logits, self_two.T, preferred_element_type=f32
    )
    returned = exchange(table_grad[node_rows:].astype(bf16), peers, slots)
    grad_hidden = local_grad + lax.dot_general(
        select, returned, (((0,), (0,)), ((), ())), preferred_element_type=f32
    )
    grad_pre = jnp.where(pre > 0.0, grad_hidden, 0.0).astype(bf16)
    grad_one = scattered(avg_one, grad_pre)
    loss = all_sum(local_total) / label_count
    return (logits, loss, grad_one, grad_two)


def solution(mesh):
    in_specs = (
        P("dom", None),
        P(),
        P(),
        P(),
        P(None, "dom", None),
        P(None, "dom", None),
        P("dom", None, None),
        P("dom", None),
        P("dom"),
    )
    out_specs = (P("dom", None), P(), P("dom", None), P("dom", None))
    return jax.shard_map(
        on_device, mesh=mesh, in_specs=in_specs, out_specs=out_specs, check_vma=False
    )
```

time: 487 us -> 331 us (0.68)
  local copies, waits for them, and re-layouts: 104 us -> 12.6 us
  other arithmetic: 80.5 us -> 7.05 us
  waiting for transfers between devices: 169 us -> 207 us
  matrix products: 60.4 us -> 33.3 us
    scatter-add x9 -> x0, other arithmetic: 56.4 us -> none  [the longest x8 52 us: add_relation(): jax.ops.segment_sum(per_edge.reshape(-1, per_edge.shape[-1]), src_rel.res...]
    gather x18 -> x0, local copies, waits for them, and re-layouts: 45.3 us -> none  [the longest x16 42 us: one_relation(): picked = node_table[src_rel]]
    psum x1 -> x0, blocking collectives: 39 us -> none  [on_device(): total, label_count = lax.psum((local_total, local_count), 'dom')]
    unnamed x0 -> x1, blocking collectives: none -> 38.7 us
    reduce_scatter x2, waiting for transfers between devices: 146 us -> 185 us  [scattered(): lax.psum_scatter(full, 'dom', scatter_dimension=0, tiled=True).astype(f32)]
    dot_general x32 -> x12, matrix products: 60.4 us -> 33.3 us  [the longest x2 8.96 us: scattered(): full = jnp.einsum('rnd,nc->rdc', left, right, preferred_element_type=f32)]
    eq x24 -> x0, local copies, waits for them, and re-layouts: 16.4 us -> none  [the longest x16 10.9 us: one_relation(): one_hot = dst_rel[:, None, :] == block_rows[None, :, None]]
    while x34 -> x0, local copies, waits for them, and re-layouts: 13.5 us -> none  [the longest x2 7.92 us: aggregate(): return lax.map(one_relation, (sources, targets))]
  transfers between devices with their start and end apart: 5 -> 5, of which waited for: 5 -> 5; matrix products, arithmetic and copies ran while one was open for 23% -> 7% of each run, Pallas kernels for 0% -> 0%
where the time goes in v1:
time: 331 us; the launch traced here: 330 us
  waiting for transfers between devices  207 us (63%)
  blocking collectives  38.7 us (12%)
  matrix products  33.3 us (10%)
  between operations  16.7 us (5%)
  starting transfers between devices  14.4 us (4%)
  local copies, waits for them, and re-layouts  12.6 us (4%)
  other arithmetic  7.05 us (2%)
    reduce_scatter x2, waiting for transfers between devices, scattered(): lax.psum_scatter(full, 'dom', scatter_dimension=0, tiled=True).astype(f32)  185 us
    unnamed x1, blocking collectives  38.7 us
    all_to_all x3, waiting for transfers between devices, exchange(): got = lax.all_to_all(sent, 'dom', split_axis=0, concat_axis=0, tiled=True)  22.5 us
    all_to_all x3, starting transfers between devices, exchange(): got = lax.all_to_all(sent, 'dom', split_axis=0, concat_axis=0, tiled=True)  14.3 us
    dot_general x2, matrix products, scattered(): full = jnp.einsum('rnd,nc->rdc', left, right, preferred_element_type=f32)  8.96 us
    unnamed x31, local copies, waits for them, and re-layouts  7.76 us
  transfers between devices with their start and end apart: 5, of which 5 were waited for; matrix products, arithmetic and copies ran while one was open for 7% of the time, Pallas kernels for 0%

profile of v1, /device:TPU:0, one launch (start us, length us, event | category | flops | bytes accessed | tf_op | source)
XLA Modules:
  0.0 329.8 jit_solution(1279392772719504101)
XLA Ops:
  8.9 1.9 convolution_bitcast_fusion.1
  10.8 7.3 %all-to-all-start = ((bf16[32,8,512]{2,1,0:T(8,128)(2,1)}), bf16[32,8,512]{2,1,0:T(8,128)(2,1)S(1)}, u32[]{:S(2)}, u32[]{:S(2)}) async-start(bf16[32,8,512]{2,1,0:T(8,128)(2,1)} %convolution_bitcast_fusion.1), calls=%async_computation | async-start | bytes 524288 | tf_op jit(solution)/shard_map/all_to_all | solution.py:13
  18.1 1.1 convert_reduce_fusion
  19.3 4.1 %fusion.7 = bf16[8,2,128,512]{3,2,1,0:T(8,128)(2,1)} fusion(s32[8,2,256]{2,1,0:T(2,128)} %param.13, s32[8,2,256]{2,1,0:T(2,128)} %param.14), kind=kOutput, calls=%fused_computation.17 | convolution fusion | flops 540540928 | bytes 2129920 | tf_op jit(solution)/shard_map/rbve,rbte->rbvt/dot_general | solution.py:38
  23.4 5.3 %all-to-all-done = bf16[32,8,512]{2,1,0:T(8,128)(2,1)S(1)} async-done(((bf16[32,8,512]{2,1,0:T(8,128)(2,1)}), bf16[32,8,512]{2,1,0:T(8,128)(2,1)S(1)}, u32[]{:S(2)}, u32[]{:S(2)}) %all-to-all-start) | async-done | bytes 262176 | tf_op jit(solution)/shard_map/all_to_all | solution.py:13
  28.7 2.8 multiply_convert_fusion.1
  31.5 5.3 %maximum_convert_fusion = (bf16[256,512]{1,0:T(8,128)(2,1)S(1)}, f32[256,512]{1,0:T(8,128)}) fusion(bf16[9,512,512]{2,1,0:T(8,128)(2,1)} %param.10, bf16[1,256,512]{2,1,0:T(8,128)(2,1)S(1)} %bitcast.57, bf16[8,256,512]{2,1,0:T(8,128)(2,1)S(1)} %bitcast.67), kind=kOutput, calls=%fused_computation.36 | convolution fusion | flops 1209401344 | bytes 7864320 | tf_op jit(solution)/shard_map/rnd,rde->ne/dot_general | solution.py:51
  37.8 3.3 %all-to-all-start.1 = ((bf16[32,8,512]{2,1,0:T(8,128)(2,1)}), bf16[32,8,512]{2,1,0:T(8,128)(2,1)}, u32[]{:S(2)}, u32[]{:S(2)}) async-start(bf16[32,8,512]{2,1,0:T(8,128)(2,1)} %convolution_bitcast_fusion), calls=%async_computation.1 | async-start | bytes 524288 | tf_op jit(solution)/shard_map/all_to_all | solution.py:13
  41.2 2.8 copy.17
  43.9 7.7 %all-to-all-done.1 = bf16[32,8,512]{2,1,0:T(8,128)(2,1)} async-done(((bf16[32,8,512]{2,1,0:T(8,128)(2,1)}), bf16[32,8,512]{2,1,0:T(8,128)(2,1)}, u32[]{:S(2)}, u32[]{:S(2)}) %all-to-all-start.1) | async-done | bytes 262176 | tf_op jit(solution)/shard_map/all_to_all | solution.py:13
  51.7 2.9 multiply_convert_fusion
  58.8 38.7 %all-reduce.2 = (f32[32]{0:T(128)S(1)}, f32[32]{0:T(128)S(1)}) all-reduce(f32[32]{0:T(128)S(1)} %dynamic-update-slice, f32[32]{0:T(128)S(1)} %dynamic-update-slice.1), channel_id=2, replica_groups=mesh['dom'=32] {'dom'}, use_global_device_ids=true, to_apply=%add | all-reduce | flops 64 | bytes 512
  98.2 3.5 %convolution_convert_fusion.1 = bf16[9,512,349]{1,2,0:T(8,128)(2,1)S(1)} fusion(bf16[1,256,512]{2,1,0:T(8,128)(2,1)} %bitcast.60, bf16[8,256,512]{2,1,0:T(8,128)(2,1)} %bitcast.73, f32[256,349]{0,1:T(8,128)} %copy-done.1, f32[]{:T(128)} %reduce_sum.69, f32[256]{0:T(256)S(1)} %get-tuple-element.11, f32[256]{0:T(256)S(1)} %get-tuple-element.10, ...), kind=kOutput, calls=%fused_computation.14 | convolution fusion | flops 826807552 | bytes 5936132 | tf_op jit(solution)/shard_map/rnd,nc->rdc/dot_general | solution.py:69
  101.6 3.9 %copy.20 = bf16[9,512,349]{2,1,0:T(8,128)(2,1)} copy(bf16[9,512,349]{1,2,0:T(8,128)(2,1)S(1)} %convolution_convert_fusion.1) | data formatting | bytes 6432768 | tf_op jit(solution)/shard_map/convert_element_type | solution.py:70
  105.6 1.7 copy-done
  107.4 2.9 fusion.1
  110.3 1.3 fusion.43
  112.4 3.7 %all-to-all-start.2 = ((bf16[32,8,512]{2,1,0:T(8,128)(2,1)}), bf16[32,8,512]{2,1,0:T(8,128)(2,1)S(1)}, u32[]{:S(2)}, u32[]{:S(2)}) async-start(bf16[32,8,512]{2,1,0:T(8,128)(2,1)} %fusion.24), calls=%async_computation.2 | async-start | bytes 524288 | tf_op jit(solution)/shard_map/all_to_all | solution.py:13
  117.1 9.5 %all-to-all-done.2 = bf16[32,8,512]{2,1,0:T(8,128)(2,1)S(1)} async-done(((bf16[32,8,512]{2,1,0:T(8,128)(2,1)}), bf16[32,8,512]{2,1,0:T(8,128)(2,1)S(1)}, u32[]{:S(2)}, u32[]{:S(2)}) %all-to-all-start.2) | async-done | bytes 262176 | tf_op jit(solution)/shard_map/all_to_all | solution.py:13
  126.6 5.5 %convolution_convert_fusion = bf16[9,512,512]{2,1,0:T(8,128)(2,1)} fusion(bf16[1,256,512]{2,1,0:T(8,128)(2,1)S(1)} %bitcast.58, bf16[8,256,512]{2,1,0:T(8,128)(2,1)} %bitcast.68, f32[256,512]{1,0:T(8,128)S(1)} %convolution_add_fusion.1, f32[256,512]{1,0:T(8,128)S(1)} %copy-done.11, bf16[32,8,512]{2,1,0:T(8,128)(2,1)S(1)} %all-to-all-done.2, ...), kind=kOutput, calls=%fused_computation.11 | convolution fusion | flops 1279197184 | bytes 8389632 | tf_op jit(solution)/shard_map/rnd,nc->rdc/dot_general | solution.py:69
  134.1 74.1 %reduce-scatter.5.cloned.1.call-done = bf16[144,349]{1,0:T(8,128)(2,1)} async-done(((bf16[4608,349]{1,0:T(8,128)(2,1)}), bf16[144,349]{1,0:T(8,128)(2,1)}) %reduce-scatter.5.cloned.1.call-update) | async-done | bytes 100528 | tf_op jit(solution)/shard_map/reduce_scatter | solution.py:71
  208.1 1.6 convert_element_type.65
  209.7 110.4 %reduce-scatter.3.cloned.1.call-done = bf16[144,512]{1,0:T(8,128)(2,1)} async-done(((bf16[4608,512]{1,0:T(8,128)(2,1)}), bf16[144,512]{1,0:T(8,128)(2,1)}) %reduce-scatter.3.cloned.1.call-update) | async-done | bytes 147472 | tf_op jit(solution)/shard_map/reduce_scatter | solution.py:71
  320.2 1.7 convert_element_type.63
  (48 shorter events, 10.0 us)
Async XLA Ops:
  10.8 17.9 %all-to-all-start = ((bf16[32,8,512]{2,1,0:T(8,128)(2,1)}), bf16[32,8,512]{2,1,0:T(8,128)(2,1)S(1)}, u32[]{:S(2)}, u32[]{:S(2)}) async-start(bf16[32,8,512]{2,1,0:T(8,128)(2,1)} %convolution_bitcast_fusion.1), calls=%async_computation | async-start | bytes 524288 | tf_op jit(solution)/shard_map/all_to_all | solution.py:13
  18.1 10.6 %copy-start.3 = (bf16[256,512]{1,0:T(8,128)(2,1)S(1)}, bf16[256,512]{1,0:T(8,128)(2,1)}, u32[]{:S(2)}) copy-start(bf16[256,512]{1,0:T(8,128)(2,1)} %param.9) | copy-start | bytes 786436
  31.5 5.3 %copy-start.8 = (bf16[2048,512]{1,0:T(8,128)(2,1)}, bf16[2048,512]{1,0:T(8,128)(2,1)S(1)}, u32[]{:S(2)}) copy-start(bf16[2048,512]{1,0:T(8,128)(2,1)S(1)} %multiply_convert_fusion.1) | copy-start | bytes 6291460
  36.8 17.8 %copy-start.4 = (bf16[256,512]{1,0:T(8,128)(2,1)}, bf16[256,512]{1,0:T(8,128)(2,1)S(1)}, u32[]{:S(2)}) copy-start(bf16[256,512]{1,0:T(8,128)(2,1)S(1)} %get-tuple-element.12) | copy-start | bytes 786436
  37.8 13.9 %all-to-all-start.1 = ((bf16[32,8,512]{2,1,0:T(8,128)(2,1)}), bf16[32,8,512]{2,1,0:T(8,128)(2,1)}, u32[]{:S(2)}, u32[]{:S(2)}) async-start(bf16[32,8,512]{2,1,0:T(8,128)(2,1)} %convolution_bitcast_fusion), calls=%async_computation.1 | async-start | bytes 524288 | tf_op jit(solution)/shard_map/all_to_all | solution.py:13
  41.1 167.0 %reduce-scatter.5.cloned.1.call-start = ((), (), s32[]{:S(2)}) async-start(), calls=%async_computation.6 | async-start | bytes 3649536 | tf_op jit(solution)/shard_map/reduce_scatter | solution.py:71
  51.7 2.9 copy-start.6
  54.6 1.3 copy-start.10
  54.6 2.0 copy-start.5
  55.9 0.7 copy-start.1
  105.5 1.8 copy-start
  105.5 1.8 copy-start.2
  107.4 3.0 copy-start.9
  110.3 5.8 %copy-start.7 = (bf16[512,349]{0,1:T(8,128)(2,1)S(1)}, bf16[512,349]{0,1:T(8,128)(2,1)}, u32[]{:S(2)}) copy-start(bf16[512,349]{0,1:T(8,128)(2,1)} %param.12) | copy-start | bytes 1072132
  111.6 15.0 %copy-start.11 = (f32[256,512]{1,0:T(8,128)S(1)}, f32[256,512]{1,0:T(8,128)}, u32[]{:S(2)}) copy-start(f32[256,512]{1,0:T(8,128)} %get-tuple-element.13) | copy-start | bytes 1572868
  112.4 14.3 %all-to-all-start.2 = ((bf16[32,8,512]{2,1,0:T(8,128)(2,1)}), bf16[32,8,512]{2,1,0:T(8,128)(2,1)S(1)}, u32[]{:S(2)}, u32[]{:S(2)}) async-start(bf16[32,8,512]{2,1,0:T(8,128)(2,1)} %fusion.24), calls=%async_computation.2 | async-start | bytes 524288 | tf_op jit(solution)/shard_map/all_to_all | solution.py:13
  116.1 204.1 %reduce-scatter.3.cloned.1.call-start = ((), (), s32[]{:S(2)}) async-start(), calls=%async_computation.5 | async-start | bytes 4866048 | tf_op jit(solution)/shard_map/reduce_scatter | solution.py:71
Sparse Core Ops, SparseCore 0:
  105.7 102.4 reduce-scatter.4
  213.6 106.5 reduce-scatter.2

commit v2 on v1

--- a/solution.py
+++ b/solution.py
@@ -1,22 +1,185 @@
+import functools
+
 import jax
 import jax.numpy as jnp
 from jax import lax
+from jax.experimental import pallas as pl
+from jax.experimental.pallas import tpu as pltpu
 from jax.sharding import PartitionSpec as P
 
 loss_scale = 256.0
 f32 = jnp.float32
 bf16 = jnp.bfloat16
-
-
-def exchange(rows, peers, slots):
-    sent = rows.reshape(peers, slots, -1)
-    got = lax.all_to_all(sent, "dom", split_axis=0, concat_axis=0, tiled=True)
-    return got.reshape(peers * slots, -1)
-
-
-def all_sum(value):
-    spread = jnp.broadcast_to(value, (1, 128))
-    return jnp.sum(lax.all_gather(spread, "dom", axis=0, tiled=True)[:, 0])
+MESH = pl.DeviceIdType.MESH
+
+
+def exchange_kernel(peers, rows_ref, stat_ref, got_ref, stats_ref, send_sem, recv_sem, stat_send, stat_recv, own_sem):
+    me = lax.axis_index("dom")
+    barrier = pltpu.get_barrier_semaphore()
+    for step in range(1, peers):
+        peer = lax.rem(me + step, peers)
+        pl.semaphore_signal(barrier, inc=1, device_id=(peer,), device_id_type=MESH)
+    own = pltpu.make_async_copy(rows_ref.at[me], got_ref.at[me], own_sem)
+    own.start()
+    stats_ref[me] = stat_ref[...]
+    pl.semaphore_wait(barrier, peers - 1)
+    copies = []
+    for step in range(1, peers):
+        peer = lax.rem(me + step, peers)
+        copies.append(
+            pltpu.make_async_remote_copy(
+                src_ref=rows_ref.at[peer],
+                dst_ref=got_ref.at[me],
+                send_sem=send_sem.at[step],
+                recv_sem=recv_sem.at[step],
+                device_id=(peer,),
+                device_id_type=MESH,
+            )
+        )
+        copies.append(
+            pltpu.make_async_remote_copy(
+                src_ref=stat_ref,
+                dst_ref=stats_ref.at[me],
+                send_sem=stat_send.at[step],
+                recv_sem=stat_recv.at[step],
+                device_id=(peer,),
+                device_id_type=MESH,
+            )
+        )
+        copies[-2].start()
+        copies[-1].start()
+    for copy in copies:
+        copy.wait_recv()
+    for copy in copies:
+        copy.wait_send()
+    own.wait()
+
+
+def exchange(rows, stat, peers, slots, call):
+    width = rows.shape[1]
+    stat = jnp.broadcast_to(stat.astype(f32), (8, 128))
+    got, stats = pl.pallas_call(
+        functools.partial(exchange_kernel, peers),
+        out_shape=[
+            jax.ShapeDtypeStruct((peers, slots, width), bf16),
+            jax.ShapeDtypeStruct((peers, 8, 128), f32),
+        ],
+        in_specs=[pl.BlockSpec(memory_space=pltpu.VMEM)] * 2,
+        out_specs=[pl.BlockSpec(memory_space=pltpu.VMEM)] * 2,
+        scratch_shapes=[pltpu.SemaphoreType.DMA((peers,))] * 4 + [pltpu.SemaphoreType.DMA],
+        compiler_params=pltpu.CompilerParams(
+            collective_id=call, has_side_effects=True, vmem_limit_bytes=8 * 1024 * 1024
+        ),
+        name=f"exchange_{call}",
+    )(rows.reshape(peers, slots, width), stat)
+    return got.reshape(peers * slots, width), jnp.sum(stats[:, 0, 0])
+
+
+def bit_orders(bits):
+    links = list(range(1, bits))
+    swapped = links[1::-1] + links[2:]
+    return links, swapped
+
+
+def placed(chunk, order):
+    spot = 0
+    for bit in order:
+        spot = spot * 2 + ((chunk >> (bit - 1)) & 1)
+    return spot
+
+
+def scatter_kernel(stripes, bits, *refs):
+    count = len(stripes)
+    parts, outs, rest = refs[:2], refs[2:4], refs[4:]
+    sums, gots, send_sem, recv_sem = rest[:bits - 1], rest[bits - 1:2 * bits - 1], rest[-2], rest[-1]
+    me = lax.axis_index("dom")
+    barrier = pltpu.get_barrier_semaphore()
+
+    def side(bit):
+        return lax.rem(me // (1 << bit), 2)
+
+    def partner(bit):
+        return me + (1 << bit) * (1 - 2 * side(bit))
+
+    for bit in range(bits):
+        pl.semaphore_signal(barrier, inc=1, device_id=(partner(bit),), device_id_type=MESH)
+    pl.semaphore_wait(barrier, bits)
+
+    def copy_of(stripe, level):
+        which, lane, order = stripes[stripe]
+        if level == 0:
+            bit = 0
+            source = parts[which].at[:, 1 - side(0), :, pl.ds(lane, 128)]
+        else:
+            bit = order[level - 1]
+            half = 1 << (bits - 1 - level)
+            source = sums[level - 1].at[stripe, pl.ds((1 - side(bit)) * half, half)]
+        return pltpu.make_async_remote_copy(
+            src_ref=source,
+            dst_ref=gots[level].at[stripe],
+            send_sem=send_sem.at[stripe, level],
+            recv_sem=recv_sem.at[stripe, level],
+            device_id=(partner(bit),),
+            device_id_type=MESH,
+        )
+
+    def add_up(stripe, level):
+        which, lane, order = stripes[stripe]
+        if level == 0:
+            for chunk in range(1 << (bits - 1)):
+                own = parts[which][chunk, side(0), :, pl.ds(lane, 128)].astype(f32)
+                total = own + gots[0][stripe, chunk].astype(f32)
+                sums[0][stripe, placed(chunk, order)] = total.astype(bf16)
+            return
+        bit = order[level - 1]
+        half = 1 << (bits - 1 - level)
+        own = sums[level - 1][stripe, pl.ds(side(bit) * half, half)].astype(f32)
+        total = own + gots[level][stripe].astype(f32)
+        if level < bits - 1:
+            sums[level][stripe] = total.astype(bf16)
+        else:
+            outs[which][:, pl.ds(lane, 128)] = total[0]
+
+    for stripe in range(count):
+        copy_of(stripe, 0).start()
+    for level in range(bits):
+        for stripe in range(count):
+            copy_of(stripe, level).wait_recv()
+            add_up(stripe, level)
+            if level < bits - 1:
+                copy_of(stripe, level + 1).start()
+    for level in range(bits):
+        for stripe in range(count):
+            copy_of(stripe, level).wait_send()
+
+
+def scatter_sums(first, second, peers):
+    bits = peers.bit_length() - 1
+    rows = first.shape[0] // peers
+    orders = bit_orders(bits)
+    stripes = []
+    for which, part in enumerate((first, second)):
+        for lane in range(0, part.shape[1], 128):
+            stripes.append((which, lane, orders[len(stripes) % 2]))
+    count = len(stripes)
+    half = peers // 2
+    sums = [pltpu.VMEM((count, half >> k, rows, 128), bf16) for k in range(bits - 1)]
+    gots = [pltpu.VMEM((count, half >> k, rows, 128), bf16) for k in range(bits)]
+    views = [part.reshape(half, 2, rows, part.shape[1]) for part in (first, second)]
+    return pl.pallas_call(
+        functools.partial(scatter_kernel, stripes, bits),
+        out_shape=[jax.ShapeDtypeStruct((rows, part.shape[1]), f32) for part in (first, second)],
+        in_specs=[pl.BlockSpec(memory_space=pltpu.VMEM)] * 2,
+        out_specs=[pl.BlockSpec(memory_space=pltpu.VMEM)] * 2,
+        scratch_shapes=sums + gots + [
+            pltpu.SemaphoreType.DMA((count, bits)),
+            pltpu.SemaphoreType.DMA((count, bits)),
+        ],
+        compiler_params=pltpu.CompilerParams(
+            collective_id=0, has_side_effects=True, vmem_limit_bytes=60 * 1024 * 1024
+        ),
+        name="scatter_sums",
+    )(*views)
 
 
 def on_device(features, w_one, w_two, self_two, edge_src, edge_dst, send_rows, send_count, labels):
@@ -26,13 +189,13 @@
     slots = send_rows.shape[2]
     table_rows = node_rows + peers * slots
     labelled = labels >= 0
-    label_count = all_sum(jnp.sum(labelled.astype(f32)))
+    local_count = jnp.sum(labelled.astype(f32))
 
     live = jnp.arange(slots, dtype=jnp.int32)[None, :] < send_count[0][:, None]
     picks = jnp.where(live, send_rows[0], -1).reshape(-1)
     select = (picks[:, None] == jnp.arange(node_rows, dtype=jnp.int32)[None, :]).astype(bf16)
 
-    arrived = exchange(jnp.dot(select, features), peers, slots)
+    arrived, label_count = exchange(jnp.dot(select, features), local_count, peers, slots, 1)
     hot_dst = edge_dst[:, :, None, :] == jnp.arange(128, dtype=jnp.int32)[None, None, :, None]
     hot_src = edge_src[:, :, None, :] == jnp.arange(table_rows, dtype=jnp.int32)[None, None, :, None]
     counts = jnp.einsum(
@@ -50,7 +213,7 @@
     avg_one = jnp.concatenate([averages(features, arrived), features[None]], axis=0)
     pre = jnp.einsum("rnd,rde->ne", avg_one, w_one, preferred_element_type=f32)
     hidden = jnp.maximum(pre, 0.0).astype(bf16)
-    arrived_hidden = exchange(jnp.dot(select, hidden), peers, slots)
+    arrived_hidden, unused = exchange(jnp.dot(select, hidden), local_count, peers, slots, 2)
     avg_two = jnp.concatenate([averages(hidden, arrived_hidden), hidden[None]], axis=0)
     w_all = jnp.concatenate([w_two, self_two[None]], axis=0)
     logits = jnp.einsum("rnd,rdc->nc", avg_two, w_all, preferred_element_type=f32)
@@ -65,26 +228,25 @@
         loss_scale * (softmax_out - one_hot) * labelled[:, None].astype(f32) / label_count
     ).astype(bf16)
 
-    def scattered(left, right):
+    def products(left, right):
         full = jnp.einsum("rnd,nc->rdc", left, right, preferred_element_type=f32)
-        full = full.astype(bf16).reshape((relations + 1) * width, -1)
-        return lax.psum_scatter(full, "dom", scatter_dimension=0, tiled=True).astype(f32)
-
-    grad_two = scattered(avg_two, grad_logits)
+        return full.astype(bf16).reshape((relations + 1) * width, -1)
+
+    padded = jnp.pad(grad_logits, ((0, 0), (0, -classes % 128)))
+    part_two = products(avg_two, padded)
     spread = jnp.einsum("nc,rdc->rnd", grad_logits, w_two, preferred_element_type=f32)
     spread = (spread.reshape(-1, width) * norm).astype(bf16)
     table_grad = lax.dot_general(adj, spread, (((0,), (0,)), ((), ())), preferred_element_type=f32)
     local_grad = table_grad[:node_rows] + jnp.dot(
         grad_logits, self_two.T, preferred_element_type=f32
     )
-    returned = exchange(table_grad[node_rows:].astype(bf16), peers, slots)
+    returned, total = exchange(table_grad[node_rows:].astype(bf16), local_total, peers, slots, 3)
     grad_hidden = local_grad + lax.dot_general(
         select, returned, (((0,), (0,)), ((), ())), preferred_element_type=f32
     )
     grad_pre = jnp.where(pre > 0.0, grad_hidden, 0.0).astype(bf16)
-    grad_one = scattered(avg_one, grad_pre)
-    loss = all_sum(local_total) / label_count
-    return (logits, loss, grad_one, grad_two)
+    grad_one, grad_two = scatter_sums(products(avg_one, grad_pre), part_two, peers)
+    return (logits, total / label_count, grad_one, grad_two[:, :classes])
 
 
 def solution(mesh):

time: 331 us -> 150 us (0.45)
  waiting for transfers between devices: 207 us -> 0 us
  Pallas kernels: 0 us -> 108 us
  blocking collectives: 38.7 us -> 0 us
  starting transfers between devices: 14.4 us -> 0 us
  between operations: 16.7 us -> 3.49 us
  matrix products: 33.3 us -> 25.4 us
  local copies, waits for them, and re-layouts: 12.6 us -> 8.13 us
    reduce_scatter x2 -> x0, waiting for transfers between devices: 185 us -> none  [scattered(): lax.psum_scatter(full, 'dom', scatter_dimension=0, tiled=True).astype(f32)]
    pallas_call x0 -> x4, Pallas kernels: none -> 108 us  [the longest x1 62 us: scatter_sums(): pl.pallas_call(functools.partial(scatter_kernel, stripes, bits), out_shap...]
    unnamed x1 -> x0, blocking collectives: 38.7 us -> none
    all_to_all x3 -> x0, waiting for transfers between devices: 22.5 us -> none  [exchange(): got = lax.all_to_all(sent, 'dom', split_axis=0, concat_axis=0, tiled=True)]
    all_to_all x3 -> x0, starting transfers between devices: 14.3 us -> none  [exchange(): got = lax.all_to_all(sent, 'dom', split_axis=0, concat_axis=0, tiled=True)]
    convert_element_type x1 -> x0, local copies, waits for them, and re-layouts: 3.88 us -> none  [scattered(): full = full.astype(bf16).reshape((relations + 1) * width, -1)]
    unnamed x31 -> x41, local copies, waits for them, and re-layouts: 7.76 us -> 6.56 us
  transfers between devices with their start and end apart: 5 -> 0, of which waited for: 5 -> 0; matrix products, arithmetic and copies ran while one was open for 7% -> 0% of each run, Pallas kernels for 0% -> 0%
where the time goes in v2:
time: 150 us; the launch traced here: 149 us
  Pallas kernels  108 us (72%)
  matrix products  25.4 us (17%)
  local copies, waits for them, and re-layouts  8.13 us (5%)
  other arithmetic  3.82 us (3%)
  between operations  3.49 us (2%)
    pallas_call x1, Pallas kernels, scatter_sums(): pl.pallas_call(functools.partial(scatter_kernel, stripes, bits), out_shap...  62 us
    pallas_call x3, Pallas kernels, exchange(): pl.pallas_call(functools.partial(exchange_kernel, peers), out_shape=[jax....  46.4 us
    dot_general x2, matrix products, products(): full = jnp.einsum('rnd,nc->rdc', left, right, preferred_element_type=f32)  10.3 us
    unnamed x41, local copies, waits for them, and re-layouts  6.56 us
    dot_general x2, matrix products, averages(): sums = jnp.dot(adj, table, preferred_element_type=f32)  4.18 us
    dot_general x1, matrix products, on_device(): jnp.einsum('rbve,rbte->rbvt', hot_dst.astype(bf16), hot_src.astype(bf16),...  3.37 us

profile of v2, /device:TPU:0, one launch (start us, length us, event | category | flops | bytes accessed | tf_op | source)
XLA Modules:
  0.0 149.2 jit_solution(9560454996310278157)
XLA Ops:
  0.7 2.8 %copy.19 = bf16[8,512,349]{1,2,0:T(8,128)(2,1)S(1)} copy(bf16[8,512,349]{1,0,2:T(8,128)(2,1)} %param.11) | data formatting | bytes 5718016 | tf_op args[2]
  3.5 3.4 %fusion.7 = bf16[8,2,128,512]{3,2,1,0:T(8,128)(2,1)} fusion(s32[8,2,256]{2,1,0:T(2,128)S(1)} %copy-done.11, s32[8,2,256]{2,1,0:T(2,128)S(1)} %copy-done.7), kind=kOutput, calls=%fused_computation.17 | convolution fusion | flops 540540928 | bytes 2129920 | tf_op jit(solution)/shard_map/rbve,rbte->rbvt/dot_general | solution.py:201
  6.9 0.4 convert_reduce_fusion
  7.9 0.6 convert_reduce_fusion.1
  8.5 0.6 broadcast_in_dim.20.stat_ref
  9.2 15.0 %exchange_1.1 = (bf16[32,8,512]{2,1,0:T(8,128)(2,1)S(1)}, f32[32,8,128]{2,1,0:T(8,128)S(1)}) custom-call(bf16[32,8,512]{2,1,0:T(8,128)(2,1)S(1)} %convolution_bitcast_fusion.1.rows_ref, f32[8,128]{1,0:T(8,128)S(1)} %broadcast_in_dim.20.stat_ref), custom_call_target="tpu_custom_call" | custom-call | tf_op jit(solution)/shard_map/exchange_1/pallas_call | solution.py:61
  24.2 2.9 %multiply_convert_fusion.1 = bf16[2048,512]{1,0:T(8,128)(2,1)S(1)} fusion(bf16[2048,512]{1,0:T(8,128)(2,1)} %bitcast.74, f32[2048]{0:T(1024)S(1)} %bitcast.66, bf16[256,512]{1,0:T(8,128)(2,1)S(1)} %bitcast.57, bf16[256,512]{1,0:T(8,128)(2,1)S(1)} %copy-done.4), kind=kOutput, calls=%fused_computation.5 | convolution fusion | flops 1076887552 | bytes 4726784 | tf_op jit(solution)/shard_map/dot_general | solution.py:210
  27.2 2.2 %maximum_convert_fusion = (bf16[256,512]{1,0:T(8,128)(2,1)S(1)}, f32[256,512]{1,0:T(8,128)}) fusion(bf16[9,512,512]{2,1,0:T(8,128)(2,1)S(1)} %bitcast.71, bf16[1,256,512]{2,1,0:T(8,128)(2,1)S(1)} %bitcast.61, bf16[8,256,512]{2,1,0:T(8,128)(2,1)S(1)} %bitcast.72), kind=kOutput, calls=%fused_computation.36 | convolution fusion | flops 1209401344 | bytes 7864320 | tf_op jit(solution)/shard_map/rnd,rde->ne/dot_general | solution.py:214
  29.7 16.0 %exchange_2.1 = (bf16[32,8,512]{2,1,0:T(8,128)(2,1)S(1)}, f32[32,8,128]{2,1,0:T(8,128)}) custom-call(bf16[32,8,512]{2,1,0:T(8,128)(2,1)S(1)} %convolution_bitcast_fusion.rows_ref, f32[8,128]{1,0:T(8,128)S(1)} %broadcast_in_dim.20.stat_ref), custom_call_target="tpu_custom_call" | custom-call | tf_op jit(solution)/shard_map/exchange_2/pallas_call | solution.py:61
  45.7 1.3 multiply_convert_fusion
  47.0 1.1 fusion.44
  48.4 0.6 slice_reduce_fusion.1
  49.2 0.6 select_reduce_fusion.1
  49.8 0.8 divide_convert_fusion
  50.6 2.2 %fusion.1 = bf16[8,256,512]{2,1,0:T(8,128)(2,1)S(1)} fusion(f32[8,256]{1,0:T(8,128)S(1)} %bitcast.68, bf16[256,349]{0,1:T(8,128)(2,1)S(1)} %divide_convert_fusion, bf16[8,512,349]{1,0,2:T(8,128)(2,1)S(1)} %copy-done), kind=kOutput, calls=%fused_computation.3 | convolution fusion | flops 734003200 | bytes 5143040 | tf_op jit(solution)/shard_map/nc,rdc->rnd/dot_general | solution.py:237
  52.8 1.3 fusion.45
  54.1 0.7 broadcast_in_dim.44.stat_ref
  54.8 15.4 %exchange_3.1 = (bf16[32,8,512]{2,1,0:T(8,128)(2,1)S(1)}, f32[32,8,128]{2,1,0:T(8,128)S(1)}) custom-call(bf16[32,8,512]{2,1,0:T(8,128)(2,1)S(1)} %fusion.24.rows_ref, f32[8,128]{1,0:T(8,128)S(1)} %broadcast_in_dim.44.stat_ref), custom_call_target="tpu_custom_call" | custom-call | tf_op jit(solution)/shard_map/exchange_3/pallas_call | solution.py:61
  70.2 0.6 slice_reduce_fusion
  72.5 5.5 %convolution_convert_fusion = bf16[9,512,512]{2,1,0:T(8,128)(2,1)} fusion(bf16[1,256,512]{2,1,0:T(8,128)(2,1)S(1)} %bitcast.62, bf16[8,256,512]{2,1,0:T(8,128)(2,1)} %bitcast.73, f32[256,512]{1,0:T(8,128)S(1)} %convolution_add_fusion.1, f32[256,512]{1,0:T(8,128)S(1)} %copy-done.15, bf16[32,8,512]{2,1,0:T(8,128)(2,1)S(1)} %get-tuple-element.15, ...), kind=kOutput, calls=%fused_computation.11 | convolution fusion | flops 1279197184 | bytes 8389632 | tf_op jit(solution)/shard_map/rnd,nc->rdc/dot_general | solution.py:232
  78.0 4.8 %convolution_convert_fusion.1 = bf16[9,512,384]{2,1,0:T(8,128)(2,1)} fusion(bf16[1,256,512]{2,1,0:T(8,128)(2,1)S(1)} %bitcast.64, bf16[8,256,512]{2,1,0:T(8,128)(2,1)} %bitcast.78, bf16[256,349]{0,1:T(8,128)(2,1)S(1)} %divide_convert_fusion), kind=kOutput, calls=%fused_computation.12 | convolution fusion | flops 908918784 | bytes 6076928 | tf_op jit(solution)/shard_map/rnd,nc->rdc/dot_general | solution.py:232
  82.8 62.0 %scatter_sums.1 = (f32[144,512]{1,0:T(8,128)}, f32[144,384]{1,0:T(8,128)}) custom-call(bf16[16,2,144,512]{3,2,1,0:T(8,128)(2,1)} %bitcast.58, bf16[16,2,144,384]{3,2,1,0:T(8,128)(2,1)} %bitcast.59), custom_call_target="tpu_custom_call" | custom-call | tf_op jit(solution)/shard_map/scatter_sums/pallas_call | solution.py:169
  144.8 1.7 %copy.35 = f32[144,512]{1,0:T(8,128)} copy(f32[144,512]{1,0:T(8,128)} %get-tuple-element.33) | data formatting | bytes 589824
  146.5 1.6 %copy.36 = f32[144,349]{1,0:T(8,128)} copy(f32[144,349]{1,0:T(8,128)} %bitcast.65) | data formatting | bytes 402048
  (51 shorter events, 1.8 us)
Async XLA Ops:
  0.6 2.8 %copy-start.7 = (s32[8,2,256]{2,1,0:T(2,128)S(1)}, s32[8,2,256]{2,1,0:T(2,128)}, u32[]{:S(2)}) copy-start(s32[8,2,256]{2,1,0:T(2,128)} %param.14) | copy-start | bytes 49156
  0.6 2.8 %copy-start.11 = (s32[8,2,256]{2,1,0:T(2,128)S(1)}, s32[8,2,256]{2,1,0:T(2,128)}, u32[]{:S(2)}) copy-start(s32[8,2,256]{2,1,0:T(2,128)} %param.13) | copy-start | bytes 49156
  3.4 3.8 %copy-start.10 = (s32[1,32]{1,0:T(1,128)S(1)}, s32[1,32]{1,0:T(1,128)}, u32[]{:S(2)}) copy-start(s32[1,32]{1,0:T(1,128)} %param.16) | copy-start | bytes 388
  3.4 4.0 %copy-start.9 = (s32[1,32,8]{1,2,0:T(8,128)S(1)}, s32[1,32,8]{1,2,0:T(8,128)}, u32[]{:S(2)}) copy-start(s32[1,32,8]{1,2,0:T(8,128)} %param.15) | copy-start | bytes 3076
  3.4 4.2 %copy-start.4 = (bf16[256,512]{1,0:T(8,128)(2,1)S(1)}, bf16[256,512]{1,0:T(8,128)(2,1)}, u32[]{:S(2)}) copy-start(bf16[256,512]{1,0:T(8,128)(2,1)} %param.9) | copy-start | bytes 786436
  3.5 4.4 %copy-start.8 = (s32[256]{0:T(256)S(1)}, s32[256]{0:T(256)}, u32[]{:S(2)}) copy-start(s32[256]{0:T(256)} %param.17) | copy-start | bytes 3076
  9.2 18.0 %slice-start = ((s8[4718592]{0:T(1024)(128)(4,1)}), s8[4194304]{0:T(1024)(128)(4,1)S(1)}, s32[]{:S(2)}) async-start(s8[4718592]{0:T(1024)(128)(4,1)} %bitcast.70), calls=%async_computation | async-start | bytes 8388608
  24.2 2.9 %slice-start.1 = ((s8[4718592]{0:T(1024)(128)(4,1)}), s8[524288]{0:T(1024)(128)(4,1)S(1)}, s32[]{:S(2)}) async-start(s8[4718592]{0:T(1024)(128)(4,1)} %bitcast.70), calls=%async_computation.1 | async-start | bytes 1048576
  27.1 2.3 %copy-start.12 = (bf16[2048,512]{1,0:T(8,128)(2,1)}, bf16[2048,512]{1,0:T(8,128)(2,1)S(1)}, u32[]{:S(2)}) copy-start(bf16[2048,512]{1,0:T(8,128)(2,1)S(1)} %multiply_convert_fusion.1) | copy-start | bytes 6291460
  27.2 18.5 %copy-start.13 = (bf16[8,2,128,512]{3,2,1,0:T(8,128)(2,1)S(1)}, bf16[8,2,128,512]{3,2,1,0:T(8,128)(2,1)}, u32[]{:S(2)}) copy-start(bf16[8,2,128,512]{3,2,1,0:T(8,128)(2,1)} %fusion.7) | copy-start | bytes 6291460
  29.4 17.6 %copy-start.5 = (bf16[256,512]{1,0:T(8,128)(2,1)}, bf16[256,512]{1,0:T(8,128)(2,1)S(1)}, u32[]{:S(2)}) copy-start(bf16[256,512]{1,0:T(8,128)(2,1)S(1)} %get-tuple-element.23) | copy-start | bytes 786436
  45.7 1.3 copy-start.2
  47.0 1.4 copy-start.14
  47.0 3.5 %copy-start = (bf16[8,512,349]{1,0,2:T(8,128)(2,1)S(1)}, bf16[8,512,349]{1,0,2:T(8,128)(2,1)}, u32[]{:S(2)}) copy-start(bf16[8,512,349]{1,0,2:T(8,128)(2,1)} %param.11) | copy-start | bytes 8577028
  48.4 4.4 %copy-start.1 = (f32[256,349]{0,1:T(8,128)}, f32[256,349]{0,1:T(8,128)S(1)}, u32[]{:S(2)}) copy-start(f32[256,349]{0,1:T(8,128)S(1)} %get-tuple-element.31) | copy-start | bytes 1072132
  52.8 19.4 %copy-start.3 = (bf16[512,349]{0,1:T(8,128)(2,1)S(1)}, bf16[512,349]{0,1:T(8,128)(2,1)}, u32[]{:S(2)}) copy-start(bf16[512,349]{0,1:T(8,128)(2,1)} %param.12) | copy-start | bytes 1072132
  54.0 18.4 %copy-start.15 = (f32[256,512]{1,0:T(8,128)S(1)}, f32[256,512]{1,0:T(8,128)}, u32[]{:S(2)}) copy-start(f32[256,512]{1,0:T(8,128)} %get-tuple-element.24) | copy-start | bytes 1572868
  72.5 5.5 %copy-start.6 = (bf16[256,512]{1,0:T(8,128)(2,1)S(1)}, bf16[256,512]{1,0:T(8,128)(2,1)}, u32[]{:S(2)}) copy-start(bf16[256,512]{1,0:T(8,128)(2,1)} %copy-done.5) | copy-start | bytes 786436

commit v3 on v2

--- a/solution.py
+++ b/solution.py
@@ -57,12 +57,12 @@
 
 def exchange(rows, stat, peers, slots, call):
     width = rows.shape[1]
-    stat = jnp.broadcast_to(stat.astype(f32), (8, 128))
+    stat = jnp.broadcast_to(stat.astype(f32), (1, 128))
     got, stats = pl.pallas_call(
         functools.partial(exchange_kernel, peers),
         out_shape=[
             jax.ShapeDtypeStruct((peers, slots, width), bf16),
-            jax.ShapeDtypeStruct((peers, 8, 128), f32),
+            jax.ShapeDtypeStruct((peers, 1, 128), f32),
         ],
         in_specs=[pl.BlockSpec(memory_space=pltpu.VMEM)] * 2,
         out_specs=[pl.BlockSpec(memory_space=pltpu.VMEM)] * 2,
@@ -78,7 +78,7 @@
 def bit_orders(bits):
     links = list(range(1, bits))
     swapped = links[1::-1] + links[2:]
-    return links, swapped
+    return links, swapped, links[2:] + links[:2]
 
 
 def placed(chunk, order):
@@ -142,12 +142,14 @@
 
     for stripe in range(count):
         copy_of(stripe, 0).start()
-    for level in range(bits):
-        for stripe in range(count):
-            copy_of(stripe, level).wait_recv()
-            add_up(stripe, level)
-            if level < bits - 1:
-                copy_of(stripe, level + 1).start()
+    units = [list(range(0, 3))] + [list(range(k, min(k + 2, count))) for k in range(3, count, 2)]
+    for wave in range(len(units) + bits - 1):
+        for level in range(bits):
+            for stripe in units[wave - level] if 0 <= wave - level < len(units) else ():
+                copy_of(stripe, level).wait_recv()
+                add_up(stripe, level)
+                if level < bits - 1:
+                    copy_of(stripe, level + 1).start()
     for level in range(bits):
         for stripe in range(count):
             copy_of(stripe, level).wait_send()
@@ -160,7 +162,7 @@
     stripes = []
     for which, part in enumerate((first, second)):
         for lane in range(0, part.shape[1], 128):
-            stripes.append((which, lane, orders[len(stripes) % 2]))
+            stripes.append((which, lane, orders[len(stripes) % 2 if stripes else 2]))
     count = len(stripes)
     half = peers // 2
     sums = [pltpu.VMEM((count, half >> k, rows, 128), bf16) for k in range(bits - 1)]

time: 150 us -> 137 us (0.913)
  Pallas kernels: 108 us -> 95.1 us
    pallas_call x1, Pallas kernels: 62 us -> 55.3 us  [scatter_sums(): pl.pallas_call(functools.partial(scatter_kernel, stripes, bits), out_shap...]
    pallas_call x3, Pallas kernels: 46.4 us -> 39.8 us  [exchange(): pl.pallas_call(functools.partial(exchange_kernel, peers), out_shape=[jax....]
where the time goes in v3:
time: 137 us; the launch traced here: 136 us
  Pallas kernels  95.1 us (69%)
  matrix products  25.4 us (19%)
  local copies, waits for them, and re-layouts  8.13 us (6%)
  other arithmetic  3.82 us (3%)
  between operations  3.49 us (3%)
    pallas_call x1, Pallas kernels, scatter_sums(): pl.pallas_call(functools.partial(scatter_kernel, stripes, bits), out_shap...  55.3 us
    pallas_call x3, Pallas kernels, exchange(): pl.pallas_call(functools.partial(exchange_kernel, peers), out_shape=[jax....  39.8 us
    dot_general x2, matrix products, products(): full = jnp.einsum('rnd,nc->rdc', left, right, preferred_element_type=f32)  10.3 us
    unnamed x41, local copies, waits for them, and re-layouts  6.56 us
    dot_general x2, matrix products, averages(): sums = jnp.dot(adj, table, preferred_element_type=f32)  4.18 us
    dot_general x1, matrix products, on_device(): jnp.einsum('rbve,rbte->rbvt', hot_dst.astype(bf16), hot_src.astype(bf16),...  3.37 us

profile of v3, /device:TPU:0, one launch (start us, length us, event | category | flops | bytes accessed | tf_op | source)
XLA Modules:
  0.0 136.0 jit_solution(5404574830151448175)
XLA Ops:
  0.7 2.8 %copy.19 = bf16[8,512,349]{1,2,0:T(8,128)(2,1)S(1)} copy(bf16[8,512,349]{1,0,2:T(8,128)(2,1)} %param.11) | data formatting | bytes 5718016 | tf_op args[2]
  3.5 3.4 %fusion.7 = bf16[8,2,128,512]{3,2,1,0:T(8,128)(2,1)} fusion(s32[8,2,256]{2,1,0:T(2,128)S(1)} %copy-done.11, s32[8,2,256]{2,1,0:T(2,128)S(1)} %copy-done.7), kind=kOutput, calls=%fused_computation.17 | convolution fusion | flops 540540928 | bytes 2129920 | tf_op jit(solution)/shard_map/rbve,rbte->rbvt/dot_general | solution.py:203
  6.9 0.4 convert_reduce_fusion
  7.9 0.6 convert_reduce_fusion.1
  8.5 0.6 broadcast_in_dim.20.stat_ref
  9.2 13.2 %exchange_1.1 = (bf16[32,8,512]{2,1,0:T(8,128)(2,1)S(1)}, f32[32,1,128]{2,1,0:T(1,128)S(1)}) custom-call(bf16[32,8,512]{2,1,0:T(8,128)(2,1)S(1)} %convolution_bitcast_fusion.1.rows_ref, f32[1,128]{1,0:T(1,128)S(1)} %broadcast_in_dim.20.stat_ref), custom_call_target="tpu_custom_call" | custom-call | tf_op jit(solution)/shard_map/exchange_1/pallas_call | solution.py:61
  22.4 2.9 %multiply_convert_fusion.1 = bf16[2048,512]{1,0:T(8,128)(2,1)S(1)} fusion(bf16[2048,512]{1,0:T(8,128)(2,1)} %bitcast.74, f32[2048]{0:T(1024)S(1)} %bitcast.66, bf16[256,512]{1,0:T(8,128)(2,1)S(1)} %bitcast.57, bf16[256,512]{1,0:T(8,128)(2,1)S(1)} %copy-done.4), kind=kOutput, calls=%fused_computation.5 | convolution fusion | flops 1076887552 | bytes 4726784 | tf_op jit(solution)/shard_map/dot_general | solution.py:212
  25.4 2.2 %maximum_convert_fusion = (bf16[256,512]{1,0:T(8,128)(2,1)S(1)}, f32[256,512]{1,0:T(8,128)}) fusion(bf16[9,512,512]{2,1,0:T(8,128)(2,1)S(1)} %bitcast.71, bf16[1,256,512]{2,1,0:T(8,128)(2,1)S(1)} %bitcast.61, bf16[8,256,512]{2,1,0:T(8,128)(2,1)S(1)} %bitcast.72), kind=kOutput, calls=%fused_computation.36 | convolution fusion | flops 1209401344 | bytes 7864320 | tf_op jit(solution)/shard_map/rnd,rde->ne/dot_general | solution.py:216
  27.9 13.6 %exchange_2.1 = (bf16[32,8,512]{2,1,0:T(8,128)(2,1)S(1)}, f32[32,1,128]{2,1,0:T(1,128)}) custom-call(bf16[32,8,512]{2,1,0:T(8,128)(2,1)S(1)} %convolution_bitcast_fusion.rows_ref, f32[1,128]{1,0:T(1,128)S(1)} %broadcast_in_dim.20.stat_ref), custom_call_target="tpu_custom_call" | custom-call | tf_op jit(solution)/shard_map/exchange_2/pallas_call | solution.py:61
  41.5 1.3 multiply_convert_fusion
  42.8 1.1 fusion.44
  44.2 0.6 slice_reduce_fusion.1
  45.0 0.6 select_reduce_fusion.1
  45.6 0.8 divide_convert_fusion
  46.4 2.2 %fusion.1 = bf16[8,256,512]{2,1,0:T(8,128)(2,1)S(1)} fusion(f32[8,256]{1,0:T(8,128)S(1)} %bitcast.68, bf16[256,349]{0,1:T(8,128)(2,1)S(1)} %divide_convert_fusion, bf16[8,512,349]{1,0,2:T(8,128)(2,1)S(1)} %copy-done), kind=kOutput, calls=%fused_computation.3 | convolution fusion | flops 734003200 | bytes 5143040 | tf_op jit(solution)/shard_map/nc,rdc->rnd/dot_general | solution.py:239
  48.6 1.3 fusion.45
  49.9 0.7 broadcast_in_dim.44.stat_ref
  50.6 13.0 %exchange_3.1 = (bf16[32,8,512]{2,1,0:T(8,128)(2,1)S(1)}, f32[32,1,128]{2,1,0:T(1,128)S(1)}) custom-call(bf16[32,8,512]{2,1,0:T(8,128)(2,1)S(1)} %fusion.24.rows_ref, f32[1,128]{1,0:T(1,128)S(1)} %broadcast_in_dim.44.stat_ref), custom_call_target="tpu_custom_call" | custom-call | tf_op jit(solution)/shard_map/exchange_3/pallas_call | solution.py:61
  63.6 0.6 slice_reduce_fusion
  66.0 5.5 %convolution_convert_fusion = bf16[9,512,512]{2,1,0:T(8,128)(2,1)} fusion(bf16[1,256,512]{2,1,0:T(8,128)(2,1)S(1)} %bitcast.62, bf16[8,256,512]{2,1,0:T(8,128)(2,1)} %bitcast.73, f32[256,512]{1,0:T(8,128)S(1)} %convolution_add_fusion.1, f32[256,512]{1,0:T(8,128)S(1)} %copy-done.15, bf16[32,8,512]{2,1,0:T(8,128)(2,1)S(1)} %get-tuple-element.15, ...), kind=kOutput, calls=%fused_computation.11 | convolution fusion | flops 1279197184 | bytes 8389632 | tf_op jit(solution)/shard_map/rnd,nc->rdc/dot_general | solution.py:234
  71.4 4.8 %convolution_convert_fusion.1 = bf16[9,512,384]{2,1,0:T(8,128)(2,1)} fusion(bf16[1,256,512]{2,1,0:T(8,128)(2,1)S(1)} %bitcast.64, bf16[8,256,512]{2,1,0:T(8,128)(2,1)} %bitcast.78, bf16[256,349]{0,1:T(8,128)(2,1)S(1)} %divide_convert_fusion), kind=kOutput, calls=%fused_computation.12 | convolution fusion | flops 908918784 | bytes 6076928 | tf_op jit(solution)/shard_map/rnd,nc->rdc/dot_general | solution.py:234
  76.2 55.3 %scatter_sums.1 = (f32[144,512]{1,0:T(8,128)}, f32[144,384]{1,0:T(8,128)}) custom-call(bf16[16,2,144,512]{3,2,1,0:T(8,128)(2,1)} %bitcast.58, bf16[16,2,144,384]{3,2,1,0:T(8,128)(2,1)} %bitcast.59), custom_call_target="tpu_custom_call" | custom-call | tf_op jit(solution)/shard_map/scatter_sums/pallas_call | solution.py:171
  131.6 1.7 %copy.35 = f32[144,512]{1,0:T(8,128)} copy(f32[144,512]{1,0:T(8,128)} %get-tuple-element.33) | data formatting | bytes 589824
  133.3 1.6 %copy.36 = f32[144,349]{1,0:T(8,128)} copy(f32[144,349]{1,0:T(8,128)} %bitcast.65) | data formatting | bytes 402048
  (51 shorter events, 1.8 us)
Async XLA Ops:
  0.6 2.8 %copy-start.7 = (s32[8,2,256]{2,1,0:T(2,128)S(1)}, s32[8,2,256]{2,1,0:T(2,128)}, u32[]{:S(2)}) copy-start(s32[8,2,256]{2,1,0:T(2,128)} %param.14) | copy-start | bytes 49156
  0.6 2.8 %copy-start.11 = (s32[8,2,256]{2,1,0:T(2,128)S(1)}, s32[8,2,256]{2,1,0:T(2,128)}, u32[]{:S(2)}) copy-start(s32[8,2,256]{2,1,0:T(2,128)} %param.13) | copy-start | bytes 49156
  3.4 3.8 %copy-start.10 = (s32[1,32]{1,0:T(1,128)S(1)}, s32[1,32]{1,0:T(1,128)}, u32[]{:S(2)}) copy-start(s32[1,32]{1,0:T(1,128)} %param.16) | copy-start | bytes 388
  3.4 4.0 %copy-start.9 = (s32[1,32,8]{1,2,0:T(8,128)S(1)}, s32[1,32,8]{1,2,0:T(8,128)}, u32[]{:S(2)}) copy-start(s32[1,32,8]{1,2,0:T(8,128)} %param.15) | copy-start | bytes 3076
  3.4 4.2 %copy-start.4 = (bf16[256,512]{1,0:T(8,128)(2,1)S(1)}, bf16[256,512]{1,0:T(8,128)(2,1)}, u32[]{:S(2)}) copy-start(bf16[256,512]{1,0:T(8,128)(2,1)} %param.9) | copy-start | bytes 786436
  3.5 4.4 %copy-start.8 = (s32[256]{0:T(256)S(1)}, s32[256]{0:T(256)}, u32[]{:S(2)}) copy-start(s32[256]{0:T(256)} %param.17) | copy-start | bytes 3076
  9.2 16.2 %slice-start = ((s8[4718592]{0:T(1024)(128)(4,1)}), s8[4194304]{0:T(1024)(128)(4,1)S(1)}, s32[]{:S(2)}) async-start(s8[4718592]{0:T(1024)(128)(4,1)} %bitcast.70), calls=%async_computation | async-start | bytes 8388608
  22.4 2.9 %slice-start.1 = ((s8[4718592]{0:T(1024)(128)(4,1)}), s8[524288]{0:T(1024)(128)(4,1)S(1)}, s32[]{:S(2)}) async-start(s8[4718592]{0:T(1024)(128)(4,1)} %bitcast.70), calls=%async_computation.1 | async-start | bytes 1048576
  25.3 2.3 %copy-start.12 = (bf16[2048,512]{1,0:T(8,128)(2,1)}, bf16[2048,512]{1,0:T(8,128)(2,1)S(1)}, u32[]{:S(2)}) copy-start(bf16[2048,512]{1,0:T(8,128)(2,1)S(1)} %multiply_convert_fusion.1) | copy-start | bytes 6291460
  25.3 16.1 %copy-start.13 = (bf16[8,2,128,512]{3,2,1,0:T(8,128)(2,1)S(1)}, bf16[8,2,128,512]{3,2,1,0:T(8,128)(2,1)}, u32[]{:S(2)}) copy-start(bf16[8,2,128,512]{3,2,1,0:T(8,128)(2,1)} %fusion.7) | copy-start | bytes 6291460
  27.6 15.2 %copy-start.5 = (bf16[256,512]{1,0:T(8,128)(2,1)}, bf16[256,512]{1,0:T(8,128)(2,1)S(1)}, u32[]{:S(2)}) copy-start(bf16[256,512]{1,0:T(8,128)(2,1)S(1)} %get-tuple-element.23) | copy-start | bytes 786436
  41.5 1.3 copy-start.2
  42.8 1.4 %copy-start.14 = (bf16[2048,512]{1,0:T(8,128)(2,1)}, bf16[2048,512]{1,0:T(8,128)(2,1)S(1)}, u32[]{:S(2)}) copy-start(bf16[2048,512]{1,0:T(8,128)(2,1)S(1)} %multiply_convert_fusion) | copy-start | bytes 6291460
  42.8 3.5 %copy-start = (bf16[8,512,349]{1,0,2:T(8,128)(2,1)S(1)}, bf16[8,512,349]{1,0,2:T(8,128)(2,1)}, u32[]{:S(2)}) copy-start(bf16[8,512,349]{1,0,2:T(8,128)(2,1)} %param.11) | copy-start | bytes 8577028
  44.2 4.4 %copy-start.1 = (f32[256,349]{0,1:T(8,128)}, f32[256,349]{0,1:T(8,128)S(1)}, u32[]{:S(2)}) copy-start(f32[256,349]{0,1:T(8,128)S(1)} %get-tuple-element.31) | copy-start | bytes 1072132
  48.6 17.0 %copy-start.3 = (bf16[512,349]{0,1:T(8,128)(2,1)S(1)}, bf16[512,349]{0,1:T(8,128)(2,1)}, u32[]{:S(2)}) copy-start(bf16[512,349]{0,1:T(8,128)(2,1)} %param.12) | copy-start | bytes 1072132
  49.9 16.1 %copy-start.15 = (f32[256,512]{1,0:T(8,128)S(1)}, f32[256,512]{1,0:T(8,128)}, u32[]{:S(2)}) copy-start(f32[256,512]{1,0:T(8,128)} %get-tuple-element.24) | copy-start | bytes 1572868
  66.0 5.5 %copy-start.6 = (bf16[256,512]{1,0:T(8,128)(2,1)S(1)}, bf16[256,512]{1,0:T(8,128)(2,1)}, u32[]{:S(2)}) copy-start(bf16[256,512]{1,0:T(8,128)(2,1)} %copy-done.5) | copy-start | bytes 786436

commit v4 on v3

--- a/solution.py
+++ b/solution.py
@@ -184,6 +184,183 @@
     )(*views)
 
 
+def tail_kernel(
+    stripes, bits, relations,
+    two_ref, back_ref, stat_ref, local_ref, pre_ref, select_ref, avg_ref,
+    one_out, two_out, stats_ref, one_ref, grad_ref, got_ref, *rest
+):
+    peers = 1 << bits
+    sums, gots = rest[:bits - 1], rest[bits - 1:2 * bits - 1]
+    send_sem, recv_sem, row_send, row_recv, stat_send, stat_recv, own_sem = rest[2 * bits - 1:]
+    parts, outs = (two_ref, one_ref), (two_out, one_out)
+    rows, width = one_ref.shape[2:]
+    me = lax.axis_index("dom")
+    barrier = pltpu.get_barrier_semaphore()
+    for step in range(1, peers):
+        peer = lax.rem(me + step, peers)
+        pl.semaphore_signal(barrier, inc=1, device_id=(peer,), device_id_type=MESH)
+    own = pltpu.make_async_copy(back_ref.at[me], got_ref.at[me], own_sem)
+    own.start()
+    stats_ref[me] = stat_ref[...]
+    pl.semaphore_wait(barrier, peers - 1)
+
+    def side(bit):
+        return lax.rem(me // (1 << bit), 2)
+
+    def copy_of(stripe, level):
+        which, lane, order = stripes[stripe]
+        if level == 0:
+            bit = 0
+            source = parts[which].at[:, 1 - side(0), :, pl.ds(lane, 128)]
+        else:
+            bit = order[level - 1]
+            half = 1 << (bits - 1 - level)
+            source = sums[level - 1].at[stripe, pl.ds((1 - side(bit)) * half, half)]
+        return pltpu.make_async_remote_copy(
+            src_ref=source,
+            dst_ref=gots[level].at[stripe],
+            send_sem=send_sem.at[stripe, level],
+            recv_sem=recv_sem.at[stripe, level],
+            device_id=(me + (1 << bit) * (1 - 2 * side(bit)),),
+            device_id_type=MESH,
+        )
+
+    def step_on(stripe, level):
+        which, lane, order = stripes[stripe]
+        copy_of(stripe, level).wait_recv()
+        if level == 0:
+            for chunk in range(1 << (bits - 1)):
+                held = parts[which][chunk, side(0), :, pl.ds(lane, 128)].astype(f32)
+                total = held + gots[0][stripe, chunk].astype(f32)
+                sums[0][stripe, placed(chunk, order)] = total.astype(bf16)
+        else:
+            bit = order[level - 1]
+            half = 1 << (bits - 1 - level)
+            held = sums[level - 1][stripe, pl.ds(side(bit) * half, half)].astype(f32)
+            total = held + gots[level][stripe].astype(f32)
+            if level < bits - 1:
+                sums[level][stripe] = total.astype(bf16)
+            else:
+                outs[which][:, pl.ds(lane, 128)] = total[0]
+        if level < bits - 1:
+            copy_of(stripe, level + 1).start()
+
+    moves = []
+    for step in range(1, peers):
+        peer = lax.rem(me + step, peers)
+        for source, target, sent, landed in (
+            (back_ref.at[peer], got_ref.at[me], row_send, row_recv),
+            (stat_ref, stats_ref.at[me], stat_send, stat_recv),
+        ):
+            move = pltpu.make_async_remote_copy(
+                src_ref=source,
+                dst_ref=target,
+                send_sem=sent.at[step],
+                recv_sem=landed.at[step],
+                device_id=(peer,),
+                device_id_type=MESH,
+            )
+            move.start()
+            moves.append(move)
+
+    early = [s for s in range(len(stripes)) if stripes[s][0] == 0]
+    late = [s for s in range(len(stripes)) if stripes[s][0] == 1]
+    units = [late[k:k + 2] for k in range(0, len(late), 2)]
+    for stripe in early:
+        copy_of(stripe, 0).start()
+    for stripe in early:
+        step_on(stripe, 0)
+    for move in moves:
+        move.wait_recv()
+    own.wait()
+    back = got_ref[...].astype(f32).reshape(-1, width).astype(bf16)
+    grad = local_ref[...] + jnp.dot(select_ref[...], back, preferred_element_type=f32)
+    grad_ref[...] = jnp.where(pre_ref[...] > 0.0, grad, 0.0).astype(bf16)
+
+    def products(unit):
+        lane, span = stripes[unit[0]][1], 128 * len(unit)
+        right = grad_ref[:, pl.ds(lane, span)]
+        for r in range(relations):
+            made = lax.dot_general(
+                avg_ref[r], right, (((0,), (0,)), ((), ())), preferred_element_type=f32
+            ).astype(bf16)
+            low = r * width
+            while low < (r + 1) * width:
+                chunk, start = low // rows, low % rows
+                size = min(rows - start, (r + 1) * width - low)
+                piece = made[low - r * width:low - r * width + size]
+                one_ref[chunk // 2, chunk % 2, pl.ds(start, size), pl.ds(lane, span)] = piece
+                low += size
+        for stripe in unit:
+            copy_of(stripe, 0).start()
+
+    done = 1
+    for unit in units:
+        for stripe in early:
+            step_on(stripe, done)
+        done += 1
+        products(unit)
+    for wave in range(bits + len(units) - 1):
+        for k, unit in enumerate(units):
+            if 0 <= wave - k < bits:
+                for stripe in unit:
+                    step_on(stripe, wave - k)
+        if done < bits:
+            for stripe in early:
+                step_on(stripe, done)
+            done += 1
+    for level in range(bits):
+        for stripe in range(len(stripes)):
+            copy_of(stripe, level).wait_send()
+    for move in moves:
+        move.wait_send()
+
+
+def tail(part_two, back, stat, local_grad, pre, select, avg_one, peers, slots):
+    bits = peers.bit_length() - 1
+    relations, nodes, width = avg_one.shape
+    rows = part_two.shape[0] // peers
+    orders = bit_orders(bits)
+    stripes = []
+    for which, columns in enumerate((part_two.shape[1], width)):
+        for lane in range(0, columns, 128):
+            stripes.append((which, lane, orders[len(stripes) % 2 if stripes else 2]))
+    count = len(stripes)
+    half = peers // 2
+    stat = jnp.broadcast_to(stat.astype(f32), (1, 128))
+    sums = [pltpu.VMEM((count, half >> k, rows, 128), bf16) for k in range(bits - 1)]
+    gots = [pltpu.VMEM((count, half >> k, rows, 128), bf16) for k in range(bits)]
+    grad_one, grad_two, stats = pl.pallas_call(
+        functools.partial(tail_kernel, stripes, bits, relations),
+        out_shape=[
+            jax.ShapeDtypeStruct((rows, width), f32),
+            jax.ShapeDtypeStruct((rows, part_two.shape[1]), f32),
+            jax.ShapeDtypeStruct((peers, 1, 128), f32),
+        ],
+        in_specs=[pl.BlockSpec(memory_space=pltpu.VMEM)] * 7,
+        out_specs=[pl.BlockSpec(memory_space=pltpu.VMEM)] * 3,
+        scratch_shapes=[
+            pltpu.VMEM((half, 2, rows, width), bf16),
+            pltpu.VMEM((nodes, width), bf16),
+            pltpu.VMEM((peers, slots, width), bf16),
+        ] + sums + gots + [pltpu.SemaphoreType.DMA((count, bits))] * 2
+        + [pltpu.SemaphoreType.DMA((peers,))] * 4 + [pltpu.SemaphoreType.DMA],
+        compiler_params=pltpu.CompilerParams(
+            collective_id=4, has_side_effects=True, vmem_limit_bytes=60 * 1024 * 1024
+        ),
+        name="tail",
+    )(
+        part_two.reshape(half, 2, rows, part_two.shape[1]),
+        back.reshape(peers, slots, width),
+        stat,
+        local_grad,
+        pre,
+        select,
+        avg_one,
+    )
+    return grad_one, grad_two, jnp.sum(stats[:, 0, 0])
+
+
 def on_device(features, w_one, w_two, self_two, edge_src, edge_dst, send_rows, send_count, labels):
     peers = lax.axis_size("dom")
     node_rows, width = features.shape
@@ -196,6 +373,8 @@
     live = jnp.arange(slots, dtype=jnp.int32)[None, :] < send_count[0][:, None]
     picks = jnp.where(live, send_rows[0], -1).reshape(-1)
     select = (picks[:, None] == jnp.arange(node_rows, dtype=jnp.int32)[None, :]).astype(bf16)
+
+    select_t = (picks[None, :] == jnp.arange(node_rows, dtype=jnp.int32)[:, None]).astype(bf16)
 
     arrived, label_count = exchange(jnp.dot(select, features), local_count, peers, slots, 1)
     hot_dst = edge_dst[:, :, None, :] == jnp.arange(128, dtype=jnp.int32)[None, None, :, None]
@@ -242,12 +421,16 @@
     local_grad = table_grad[:node_rows] + jnp.dot(
         grad_logits, self_two.T, preferred_element_type=f32
     )
-    returned, total = exchange(table_grad[node_rows:].astype(bf16), local_total, peers, slots, 3)
-    grad_hidden = local_grad + lax.dot_general(
-        select, returned, (((0,), (0,)), ((), ())), preferred_element_type=f32
-    )
-    grad_pre = jnp.where(pre > 0.0, grad_hidden, 0.0).astype(bf16)
-    grad_one, grad_two = scatter_sums(products(avg_one, grad_pre), part_two, peers)
+    back = table_grad[node_rows:].astype(bf16)
+    if (relations + 1) * width // peers % 16 == 0:
+        grad_one, grad_two, total = tail(
+            part_two, back, local_total, local_grad, pre, select_t, avg_one, peers, slots
+        )
+    else:
+        returned, total = exchange(back, local_total, peers, slots, 3)
+        grad_hidden = local_grad + jnp.dot(select_t, returned, preferred_element_type=f32)
+        grad_pre = jnp.where(pre > 0.0, grad_hidden, 0.0).astype(bf16)
+        grad_one, grad_two = scatter_sums(products(avg_one, grad_pre), part_two, peers)
     return (logits, total / label_count, grad_one, grad_two[:, :classes])
 
 

time: 137 us -> 131 us (0.956)
  matrix products: 25.4 us -> 18 us
  other arithmetic: 3.82 us -> 8.22 us
  Pallas kernels: 95.1 us -> 92.4 us
    pallas_call x3 -> x2, Pallas kernels: 39.8 us -> 26.8 us  [exchange(): pl.pallas_call(functools.partial(exchange_kernel, peers), out_shape=[jax....]
    pallas_call x1, Pallas kernels: 55.3 us -> 65.6 us  [tail(): pl.pallas_call(functools.partial(tail_kernel, stripes, bits, relations),...]
    dot_general x2 -> x1, matrix products: 10.3 us -> 3.22 us  [products(): full = jnp.einsum('rnd,nc->rdc', left, right, preferred_element_type=f32)]
    concatenate x0 -> x1, other arithmetic: none -> 1.63 us  [on_device(): jnp.concatenate([averages(features, arrived), features[None]], axis=0)]
    dot_general x2, matrix products: 4.18 us -> 2.55 us  [averages(): sums = jnp.dot(adj, table, preferred_element_type=f32)]
    unnamed x41 -> x21, local copies, waits for them, and re-layouts: 6.56 us -> 5.64 us
where the time goes in v4:
time: 131 us; the launch traced here: 130 us
  Pallas kernels  92.4 us (71%)
  matrix products  18 us (14%)
  local copies, waits for them, and re-layouts  8.35 us (6%)
  other arithmetic  8.22 us (6%)
  between operations  3.33 us (3%)
    pallas_call x1, Pallas kernels, tail(): pl.pallas_call(functools.partial(tail_kernel, stripes, bits, relations),...  65.6 us
    pallas_call x2, Pallas kernels, exchange(): pl.pallas_call(functools.partial(exchange_kernel, peers), out_shape=[jax....  26.8 us
    unnamed x21, local copies, waits for them, and re-layouts  5.64 us
    dot_general x1, matrix products, products(): full = jnp.einsum('rnd,nc->rdc', left, right, preferred_element_type=f32)  3.22 us
    dot_general x1, matrix products, on_device(): jnp.einsum('rbve,rbte->rbvt', hot_dst.astype(bf16), hot_src.astype(bf16),...  2.94 us

profile of v4, /device:TPU:0, one launch (start us, length us, event | category | flops | bytes accessed | tf_op | source)
XLA Modules:
  0.0 130.3 jit_solution(10445768260989115046)
XLA Ops:
  0.6 0.8 copy.17
  1.5 0.7 iota_compare_fusion.13
  2.3 1.2 convolution_bitcast_fusion.2.rows_ref
  3.6 1.3 convert_reduce_fusion.1
  5.5 13.2 %exchange_1.1 = (bf16[32,8,512]{2,1,0:T(8,128)(2,1)S(1)}, f32[32,1,128]{2,1,0:T(1,128)S(1)}) custom-call(bf16[32,8,512]{2,1,0:T(8,128)(2,1)S(1)} %convolution_bitcast_fusion.2.rows_ref, f32[1,128]{1,0:T(1,128)S(1)} %broadcast_in_dim.18.stat_ref), custom_call_target="tpu_custom_call" | custom-call | tf_op jit(solution)/shard_map/exchange_1/pallas_call | solution.py:61
  18.8 2.9 %fusion.7 = bf16[8,2,128,512]{3,2,1,0:T(8,128)(2,1)S(1)} fusion(s32[8,2,256]{2,1,0:T(2,128)} %param.13, s32[8,2,256]{2,1,0:T(2,128)} %param.14), kind=kOutput, calls=%fused_computation.16 | convolution fusion | flops 540540928 | bytes 2129920 | tf_op jit(solution)/shard_map/rbve,rbte->rbvt/dot_general | solution.py:382
  22.1 1.3 multiply_convert_fusion.1
  23.4 2.2 %maximum_convert_fusion = (bf16[256,512]{1,0:T(8,128)(2,1)S(1)}, f32[256,512]{1,0:T(8,128)}) fusion(bf16[9,512,512]{2,1,0:T(8,128)(2,1)S(1)} %bitcast.63, bf16[1,256,512]{2,1,0:T(8,128)(2,1)S(1)} %bitcast.52, bf16[8,256,512]{2,1,0:T(8,128)(2,1)S(1)} %bitcast.50), kind=kOutput, calls=%fused_computation.30 | convolution fusion | flops 1209401344 | bytes 7864320 | tf_op jit(solution)/shard_map/rnd,rde->ne/dot_general | solution.py:395
  25.9 13.6 %exchange_2.1 = (bf16[32,8,512]{2,1,0:T(8,128)(2,1)S(1)}, f32[32,1,128]{2,1,0:T(1,128)}) custom-call(bf16[32,8,512]{2,1,0:T(8,128)(2,1)S(1)} %convolution_bitcast_fusion.1.rows_ref, f32[1,128]{1,0:T(1,128)S(1)} %broadcast_in_dim.18.stat_ref), custom_call_target="tpu_custom_call" | custom-call | tf_op jit(solution)/shard_map/exchange_2/pallas_call | solution.py:61
  39.5 1.3 multiply_convert_fusion
  41.4 0.9 copy.18
  42.3 1.1 fusion.31
  44.8 0.8 divide_convert_fusion
  45.6 2.1 %fusion.1 = bf16[8,256,512]{2,1,0:T(8,128)(2,1)S(1)} fusion(f32[8,256]{1,0:T(8,128)S(1)} %bitcast.60, bf16[256,349]{0,1:T(8,128)(2,1)S(1)} %divide_convert_fusion, bf16[8,512,349]{1,0,2:T(8,128)(2,1)S(1)} %copy-done), kind=kOutput, calls=%fused_computation.3 | convolution fusion | flops 734003200 | bytes 5143040 | tf_op jit(solution)/shard_map/nc,rdc->rnd/dot_general | solution.py:418
  47.7 1.3 fusion.32
  49.0 1.1 convolution_add_fusion.local_ref
  50.1 0.7 fusion.18.back_ref
  50.9 3.2 %convolution_convert_fusion = bf16[9,512,384]{2,1,0:T(8,128)(2,1)} fusion(bf16[1,256,512]{2,1,0:T(8,128)(2,1)S(1)} %bitcast.56, bf16[8,256,512]{2,1,0:T(8,128)(2,1)S(1)} %bitcast.68, bf16[256,349]{0,1:T(8,128)(2,1)S(1)} %divide_convert_fusion), kind=kOutput, calls=%fused_computation.11 | convolution fusion | flops 908918784 | bytes 6076928 | tf_op jit(solution)/shard_map/rnd,nc->rdc/dot_general | solution.py:413
  54.1 1.1 broadcast_in_dim.43.stat_ref
  55.2 1.6 %pad_maximum_fusion.avg_ref = bf16[9,256,512]{2,1,0:T(8,128)(2,1)} fusion(bf16[1,256,512]{2,1,0:T(8,128)(2,1)S(1)} %bitcast.53, bf16[8,256,512]{2,1,0:T(8,128)(2,1)S(1)} %bitcast.51), kind=kLoop, calls=%fused_computation.12 | loop fusion | flops 1179648 | bytes 4718592 | tf_op jit(solution)/shard_map/concatenate | solution.py:394
  57.5 65.6 %tail.1 = (f32[144,512]{1,0:T(8,128)}, f32[144,384]{1,0:T(8,128)}, f32[32,1,128]{2,1,0:T(1,128)}) custom-call(bf16[16,2,144,384]{3,2,1,0:T(8,128)(2,1)} %bitcast.49, bf16[32,8,512]{2,1,0:T(8,128)(2,1)} %fusion.18.back_ref, f32[1,128]{1,0:T(1,128)} %broadcast_in_dim.43.stat_ref, f32[256,512]{1,0:T(8,128)} %convolution_add_fusion.local_ref, ...), custom_call_target="tpu_custom_call" | custom-call | tf_op jit(solution)/shard_map/tail/pallas_call | solution.py:333
  123.1 1.4 %slice_reduce_fusion = f32[]{:T(128)} fusion(f32[32,1,128]{2,1,0:T(1,128)} %get-tuple-element.13), kind=kLoop, calls=%fused_computation.44 | loop fusion | flops 31 | bytes 132 | tf_op jit(solution)/shard_map/reduce_sum | solution.py:361
  125.8 1.7 %copy.32 = f32[144,512]{1,0:T(8,128)} copy(f32[144,512]{1,0:T(8,128)} %get-tuple-element.31) | data formatting | bytes 589824
  127.5 1.6 %copy.33 = f32[144,349]{1,0:T(8,128)} copy(f32[144,349]{1,0:T(8,128)} %bitcast.57) | data formatting | bytes 402048
  (31 shorter events, 4.1 us)
Async XLA Ops:
  3.5 18.1 %copy-start.4 = (s32[8,2,256]{2,1,0:T(2,128)S(1)}, s32[8,2,256]{2,1,0:T(2,128)}, u32[]{:S(2)}) copy-start(s32[8,2,256]{2,1,0:T(2,128)} %param.14) | copy-start | bytes 49156
  5.5 16.6 %copy-start.2 = (bf16[256,512]{1,0:T(8,128)(2,1)S(1)}, bf16[256,512]{1,0:T(8,128)(2,1)}, u32[]{:S(2)}) copy-start(bf16[256,512]{1,0:T(8,128)(2,1)} %param.9) | copy-start | bytes 786436
  18.7 4.7 %slice-start = ((s8[4718592]{0:T(1024)(128)(4,1)}), s8[4194304]{0:T(1024)(128)(4,1)S(1)}, s32[]{:S(2)}) async-start(s8[4718592]{0:T(1024)(128)(4,1)} %bitcast.62), calls=%async_computation | async-start | bytes 8388608
  22.1 1.3 %slice-start.1 = ((s8[4718592]{0:T(1024)(128)(4,1)}), s8[524288]{0:T(1024)(128)(4,1)S(1)}, s32[]{:S(2)}) async-start(s8[4718592]{0:T(1024)(128)(4,1)} %bitcast.62), calls=%async_computation.1 | async-start | bytes 1048576
  39.5 1.8 %copy-start = (bf16[8,512,349]{1,0,2:T(8,128)(2,1)S(1)}, bf16[8,512,349]{1,0,2:T(8,128)(2,1)}, u32[]{:S(2)}) copy-start(bf16[8,512,349]{1,0,2:T(8,128)(2,1)} %param.11) | copy-start | bytes 8577028
  41.3 1.0 copy-start.3
  42.3 1.1 copy-start.5
  43.4 4.3 %copy-start.1 = (f32[256,349]{0,1:T(8,128)}, f32[256,349]{0,1:T(8,128)S(1)}, u32[]{:S(2)}) copy-start(f32[256,349]{0,1:T(8,128)S(1)} %get-tuple-element.29) | copy-start | bytes 1072132

commit v5 on v4

--- a/solution.py
+++ b/solution.py
@@ -13,7 +13,31 @@
 MESH = pl.DeviceIdType.MESH
 
 
-def exchange_kernel(peers, rows_ref, stat_ref, got_ref, stats_ref, send_sem, recv_sem, stat_send, stat_recv, own_sem):
+def build_counts(src_ref, dst_ref, adj_ref, norm_ref):
+    relations, blocks, edges = src_ref.shape
+    table_rows = adj_ref.shape[1]
+    block_rows = lax.broadcasted_iota(jnp.int32, (128, edges), 0)
+    sources = lax.broadcasted_iota(jnp.int32, (table_rows, edges), 0)
+    for r in range(relations):
+        for b in range(blocks):
+            hot_dst = jnp.where(block_rows == dst_ref[r, pl.ds(b, 1), :], 1.0, 0.0)
+            hot_src = jnp.where(sources == src_ref[r, pl.ds(b, 1), :], 1.0, 0.0).astype(bf16)
+            counts = lax.dot_general(
+                hot_dst.astype(bf16), hot_src, (((1,), (1,)), ((), ())), preferred_element_type=f32
+            )
+            spot = pl.ds((r * blocks + b) * 128, 128)
+            adj_ref[spot, :] = counts.astype(bf16)
+            norm_ref[spot, :] = 1.0 / jnp.maximum(jnp.sum(hot_dst, axis=1, keepdims=True), 1.0)
+
+
+def first_kernel(peers, rows_ref, stat_ref, src_ref, dst_ref, got_ref, stats_ref, adj_ref, norm_ref, *sems):
+    def beside():
+        build_counts(src_ref, dst_ref, adj_ref, norm_ref)
+
+    exchange_kernel(peers, rows_ref, stat_ref, got_ref, stats_ref, *sems, beside=beside)
+
+
+def exchange_kernel(peers, rows_ref, stat_ref, got_ref, stats_ref, send_sem, recv_sem, stat_send, stat_recv, own_sem, beside=None):
     me = lax.axis_index("dom")
     barrier = pltpu.get_barrier_semaphore()
     for step in range(1, peers):
@@ -48,6 +72,8 @@
         )
         copies[-2].start()
         copies[-1].start()
+    if beside is not None:
+        beside()
     for copy in copies:
         copy.wait_recv()
     for copy in copies:
@@ -55,24 +81,32 @@
     own.wait()
 
 
-def exchange(rows, stat, peers, slots, call):
+def exchange(rows, stat, peers, slots, call, edge_pair=()):
     width = rows.shape[1]
+    made = []
+    if edge_pair:
+        targets = edge_pair[0].shape[0] * edge_pair[0].shape[1] * 128
+        table_rows = targets // edge_pair[0].shape[0] + peers * slots
+        made = [
+            jax.ShapeDtypeStruct((targets, table_rows), bf16),
+            jax.ShapeDtypeStruct((targets, 1), f32),
+        ]
     stat = jnp.broadcast_to(stat.astype(f32), (1, 128))
-    got, stats = pl.pallas_call(
-        functools.partial(exchange_kernel, peers),
+    got, stats, *made = pl.pallas_call(
+        functools.partial(first_kernel if edge_pair else exchange_kernel, peers),
         out_shape=[
             jax.ShapeDtypeStruct((peers, slots, width), bf16),
             jax.ShapeDtypeStruct((peers, 1, 128), f32),
-        ],
-        in_specs=[pl.BlockSpec(memory_space=pltpu.VMEM)] * 2,
-        out_specs=[pl.BlockSpec(memory_space=pltpu.VMEM)] * 2,
+        ] + made,
+        in_specs=[pl.BlockSpec(memory_space=pltpu.VMEM)] * (2 + len(edge_pair)),
+        out_specs=[pl.BlockSpec(memory_space=pltpu.VMEM)] * (2 + len(made)),
         scratch_shapes=[pltpu.SemaphoreType.DMA((peers,))] * 4 + [pltpu.SemaphoreType.DMA],
         compiler_params=pltpu.CompilerParams(
-            collective_id=call, has_side_effects=True, vmem_limit_bytes=8 * 1024 * 1024
+            collective_id=call, has_side_effects=True, vmem_limit_bytes=(32 if edge_pair else 8) * 1024 * 1024
         ),
         name=f"exchange_{call}",
-    )(rows.reshape(peers, slots, width), stat)
-    return got.reshape(peers * slots, width), jnp.sum(stats[:, 0, 0])
+    )(rows.reshape(peers, slots, width), stat, *edge_pair)
+    return (got.reshape(peers * slots, width), jnp.sum(stats[:, 0, 0]), *made)
 
 
 def bit_orders(bits):
@@ -376,16 +410,9 @@
 
     select_t = (picks[None, :] == jnp.arange(node_rows, dtype=jnp.int32)[:, None]).astype(bf16)
 
-    arrived, label_count = exchange(jnp.dot(select, features), local_count, peers, slots, 1)
-    hot_dst = edge_dst[:, :, None, :] == jnp.arange(128, dtype=jnp.int32)[None, None, :, None]
-    hot_src = edge_src[:, :, None, :] == jnp.arange(table_rows, dtype=jnp.int32)[None, None, :, None]
-    counts = jnp.einsum(
-        "rbve,rbte->rbvt", hot_dst.astype(bf16), hot_src.astype(bf16), preferred_element_type=f32
+    arrived, label_count, adj, norm = exchange(
+        jnp.dot(select, features), local_count, peers, slots, 1, (edge_src, edge_dst)
     )
-    adj = counts.astype(bf16).reshape(relations * blocks * 128, table_rows)
-    norm = 1.0 / jnp.maximum(jnp.sum(hot_dst.astype(f32), axis=3), 1.0)
-    norm = norm.reshape(relations * blocks * 128, 1)
-
     def averages(own, got):
         table = jnp.concatenate([own, got], axis=0)
         sums = jnp.dot(adj, table, preferred_element_type=f32)

time: 131 us -> 133 us (1.015)
  local copies, waits for them, and re-layouts: 8.35 us -> 9.75 us
    dot_general x1 -> x0, matrix products: 2.94 us -> none  [on_device(): jnp.einsum('rbve,rbte->rbvt', hot_dst.astype(bf16), hot_src.astype(bf16),...]
    dot_general x1, matrix products: 2.22 us -> 4.51 us  [on_device(): pre = jnp.einsum('rnd,rde->ne', avg_one, w_one, preferred_element_type=f32)]
    unnamed x21 -> x18, local copies, waits for them, and re-layouts: 5.64 us -> 7.04 us
where the time goes in v5:
time: 133 us; the launch traced here: 132 us
  Pallas kernels  92.3 us (69%)
  matrix products  18.3 us (14%)
  local copies, waits for them, and re-layouts  9.75 us (7%)
  other arithmetic  8.51 us (6%)
  between operations  3.26 us (2%)
    pallas_call x1, Pallas kernels, tail(): pl.pallas_call(functools.partial(tail_kernel, stripes, bits, relations),...  65.6 us
    pallas_call x2, Pallas kernels, exchange(): pl.pallas_call(functools.partial(first_kernel if edge_pair else exchange_...  26.8 us
    unnamed x18, local copies, waits for them, and re-layouts  7.04 us
    dot_general x1, matrix products, on_device(): pre = jnp.einsum('rnd,rde->ne', avg_one, w_one, preferred_element_type=f32)  4.51 us
    dot_general x2, matrix products, averages(): sums = jnp.dot(adj, table, preferred_element_type=f32)  3.57 us
    dot_general x1, matrix products, products(): full = jnp.einsum('rnd,nc->rdc', left, right, preferred_element_type=f32)  3.22 us

profile of v5, /device:TPU:0, one launch (start us, length us, event | category | flops | bytes accessed | tf_op | source)
XLA Modules:
  0.0 132.2 jit_solution(16760431728941728321)
XLA Ops:
  0.6 0.8 copy.17
  1.5 0.7 iota_compare_fusion.5
  2.3 1.2 convolution_bitcast_fusion.2.rows_ref
  3.5 1.3 convert_reduce_fusion
  6.2 0.7 copy-done.1
  6.9 13.2 %exchange_1.1 = (bf16[32,8,512]{2,1,0:T(8,128)(2,1)S(1)}, f32[32,1,128]{2,1,0:T(1,128)S(1)}, bf16[2048,512]{1,0:T(8,128)(2,1)S(1)}, f32[2048,1]{1,0:T(8,128)S(1)}) custom-call(bf16[32,8,512]{2,1,0:T(8,128)(2,1)S(1)} %convolution_bitcast_fusion.2.rows_ref, f32[1,128]{1,0:T(1,128)S(1)} %broadcast_in_dim.34.stat_ref, s32[8,2,256]{2,1,0:T(2,128)S(1)} %copy-done, ...), custom_call_target="tpu_custom_call" | custom-call | tf_op jit(solution)/shard_map/exchange_1/pallas_call | solution.py:95
  20.5 2.3 %multiply_convert_fusion.1 = bf16[2048,512]{1,0:T(8,128)(2,1)S(1)} fusion(bf16[2048,512]{1,0:T(8,128)(2,1)S(1)} %get-tuple-element.12, f32[2048]{0:T(1024)S(1)} %reduce.2, bf16[256,512]{1,0:T(8,128)(2,1)S(1)} %bitcast.41, bf16[256,512]{1,0:T(8,128)(2,1)} %param.9), kind=kOutput, calls=%fused_computation.3 | convolution fusion | flops 1076887552 | bytes 4726784 | tf_op jit(solution)/shard_map/dot_general | solution.py:418
  22.8 4.5 %maximum_convert_fusion = (bf16[256,512]{1,0:T(8,128)(2,1)S(1)}, f32[256,512]{1,0:T(8,128)}) fusion(bf16[9,512,512]{2,1,0:T(8,128)(2,1)} %param.10, bf16[1,256,512]{2,1,0:T(8,128)(2,1)S(1)} %bitcast.46, bf16[8,256,512]{2,1,0:T(8,128)(2,1)S(1)} %bitcast.44), kind=kOutput, calls=%fused_computation.23 | convolution fusion | flops 1209401344 | bytes 7864320 | tf_op jit(solution)/shard_map/rnd,rde->ne/dot_general | solution.py:422
  27.6 13.6 %exchange_2.1 = (bf16[32,8,512]{2,1,0:T(8,128)(2,1)S(1)}, f32[32,1,128]{2,1,0:T(1,128)}) custom-call(bf16[32,8,512]{2,1,0:T(8,128)(2,1)S(1)} %convolution_bitcast_fusion.1.rows_ref, f32[1,128]{1,0:T(1,128)S(1)} %broadcast_in_dim.34.stat_ref), custom_call_target="tpu_custom_call" | custom-call | tf_op jit(solution)/shard_map/exchange_2/pallas_call | solution.py:95
  41.2 1.3 multiply_convert_fusion
  43.0 0.9 copy.18
  44.0 1.1 fusion.28
  46.4 0.8 divide_convert_fusion
  47.2 2.1 %fusion.18 = f32[256,8,512]{2,0,1:T(8,128)S(1)} fusion(bf16[256,349]{0,1:T(8,128)(2,1)S(1)} %divide_convert_fusion, bf16[8,512,349]{1,0,2:T(8,128)(2,1)S(1)} %copy-done.2), kind=kOutput, calls=%fused_computation.34 | convolution fusion | flops 731906048 | bytes 7232000 | tf_op jit(solution)/shard_map/nc,rdc->rnd/dot_general | solution.py:445
  49.6 1.3 fusion.29
  50.9 1.1 convolution_add_fusion.local_ref
  52.0 0.7 fusion.14.back_ref
  52.8 3.2 %convolution_convert_fusion = bf16[9,512,384]{2,1,0:T(8,128)(2,1)} fusion(bf16[1,256,512]{2,1,0:T(8,128)(2,1)S(1)} %bitcast.50, bf16[8,256,512]{2,1,0:T(8,128)(2,1)S(1)} %bitcast.54, bf16[256,349]{0,1:T(8,128)(2,1)S(1)} %divide_convert_fusion), kind=kOutput, calls=%fused_computation.8 | convolution fusion | flops 908918784 | bytes 6076928 | tf_op jit(solution)/shard_map/rnd,nc->rdc/dot_general | solution.py:440
  56.0 1.1 broadcast_in_dim.39.stat_ref
  57.1 1.6 %pad_maximum_fusion.avg_ref = bf16[9,256,512]{2,1,0:T(8,128)(2,1)} fusion(bf16[1,256,512]{2,1,0:T(8,128)(2,1)S(1)} %bitcast.47, bf16[8,256,512]{2,1,0:T(8,128)(2,1)S(1)} %bitcast.45), kind=kLoop, calls=%fused_computation.9 | loop fusion | flops 1179648 | bytes 4718592 | tf_op jit(solution)/shard_map/concatenate | solution.py:421
  59.5 65.6 %tail.1 = (f32[144,512]{1,0:T(8,128)}, f32[144,384]{1,0:T(8,128)}, f32[32,1,128]{2,1,0:T(1,128)}) custom-call(bf16[16,2,144,384]{3,2,1,0:T(8,128)(2,1)} %bitcast.43, bf16[32,8,512]{2,1,0:T(8,128)(2,1)} %fusion.14.back_ref, f32[1,128]{1,0:T(1,128)} %broadcast_in_dim.39.stat_ref, f32[256,512]{1,0:T(8,128)} %convolution_add_fusion.local_ref, ...), custom_call_target="tpu_custom_call" | custom-call | tf_op jit(solution)/shard_map/tail/pallas_call | solution.py:367
  125.0 1.4 %slice_reduce_fusion = f32[]{:T(128)} fusion(f32[32,1,128]{2,1,0:T(1,128)} %get-tuple-element.17), kind=kLoop, calls=%fused_computation.38 | loop fusion | flops 31 | bytes 132 | tf_op jit(solution)/shard_map/reduce_sum | solution.py:395
  127.7 1.7 %copy.29 = f32[144,512]{1,0:T(8,128)} copy(f32[144,512]{1,0:T(8,128)} %get-tuple-element.35) | data formatting | bytes 589824
  129.4 1.6 %copy.30 = f32[144,349]{1,0:T(8,128)} copy(f32[144,349]{1,0:T(8,128)} %bitcast.51) | data formatting | bytes 402048
  (25 shorter events, 5.1 us)
Async XLA Ops:
  5.5 0.7 copy-start
  6.2 0.7 copy-start.1
  20.5 2.3 %copy-start.4 = (bf16[256,512]{1,0:T(8,128)(2,1)S(1)}, bf16[256,512]{1,0:T(8,128)(2,1)}, u32[]{:S(2)}) copy-start(bf16[256,512]{1,0:T(8,128)(2,1)} %param.9) | copy-start | bytes 786436
  41.2 1.8 %copy-start.2 = (bf16[8,512,349]{1,0,2:T(8,128)(2,1)S(1)}, bf16[8,512,349]{1,0,2:T(8,128)(2,1)}, u32[]{:S(2)}) copy-start(bf16[8,512,349]{1,0,2:T(8,128)(2,1)} %param.11) | copy-start | bytes 8577028
  43.0 1.0 copy-start.5
  43.9 1.1 copy-start.6
  45.0 4.2 %copy-start.3 = (f32[256,349]{0,1:T(8,128)}, f32[256,349]{0,1:T(8,128)S(1)}, u32[]{:S(2)}) copy-start(f32[256,349]{0,1:T(8,128)S(1)} %get-tuple-element.33) | copy-start | bytes 1072132
